TPU v7x, 128 devices: a whole 4x4x4 slice. The times are simulated.
128 devices in a mesh: dp: 16 (over z, y), tp: 8 (over x, core).
Axes of the slice: x: 4, y: 4, z: 4, core: 2. Of those that a mesh axis runs over, the one named last changes fastest.
Arguments:
- q_latent: bfloat16 [2048, 4, 1536], P('dp'), may hold values from -6 to 6
- new_latent: bfloat16 [2048, 4, 512], P('dp'), may hold values from -6 to 6
- new_rope: bfloat16 [2048, 4, 64], P('dp'), may hold values from -6 to 6
- cache_latent: bfloat16 [2048, 256, 512], P('dp'), may hold values from -6 to 6
- cache_rope: bfloat16 [2048, 64, 256], P('dp'), may hold values from -1200 to 1200
- lengths: int32 [2048], P('dp'), may hold values from 1 to 256
- assignment: int32 [16, 128], P('dp'), may hold values from 0 to 127, each once within a row
- w_uq: float32 [1536, 12288], P(('dp', 'tp')), may hold values from -0.15625 to 0.15625
- w_uk: float32 [512, 8192], P(('dp', 'tp')), may hold values from -3 to 3
- w_uv: float32 [512, 8192], P(('dp', 'tp')), may hold values from -0.25 to 0.25
- w_o: float32 [8192, 7168], P(None, ('dp', 'tp')), may hold values from -0.0625 to 0.0625
Outputs:
- attention_out: bfloat16 [2048, 4, 7168], P('dp', None, 'tp')
- weight_norm: float32 [1], replicated
Inputs may be any that keep to these rules, and one draw needn't show every extreme that they name: Each row of assignment is a permutation of 0 to 127.
All inputs are finite; a program needn't handle non-finite values.
Results may differ from a plain program's by a relative error of at most 0.006.
The roundings to bfloat16 on the way count: a program that leaves them out, or rounds other values in their place, can miss the bound.
Values may be sent and summed in bfloat16 or wider, within the bound.
A program may use at most 256 MiB of HBM per device.

v0:
```python
import jax
import jax.numpy as jnp
from jax import lax
from jax.sharding import Mesh
from jax.sharding import PartitionSpec as P

D = 7168
QRANK = 1536
KVRANK = 512
NOPE = 128
ROPE = 64
VDIM = 128
HEADS = 64
NEWTOK = 4
CACHE = 256
DP_TP = ("dp_0", "dp_1", "tp_0", "tp_1")
TP = ("tp_0", "tp_1")
DP = ("dp_0", "dp_1")


def over_axes(value, axes):
    for axis in axes:
        value = lax.psum(value, axis)
    return value


def joined_along(tiles, dim):
    lengths = list(tiles.shape[1:])
    lengths[dim] *= tiles.shape[0]
    return jnp.moveaxis(tiles, 0, dim).reshape(lengths)


def gather_together(arrays, axis, dims):
    ravelled = jnp.concatenate([a.reshape(-1) for a in arrays])
    lines, at, finished = (lax.all_gather(ravelled, axis), 0, [])
    for a, dim in zip(arrays, dims):
        tiles = lines[:, at : at + a.size].reshape(-1, *a.shape)
        finished.append(joined_along(tiles, dim))
        at += a.size
    return tuple(finished)


def widen(values):
    return lax.optimization_barrier(values).astype(jnp.float32)


def rotate_half(values, positions):
    half_width = values.shape[-1] // 2
    frequency = 10000.0 ** (-jnp.arange(half_width, dtype=jnp.float32) / half_width)
    angles = positions.astype(jnp.float32)[:, :, None, None] * frequency
    cosine = jnp.cos(angles)
    sine_part = jnp.sin(angles)
    lower_half = values[..., :half_width]
    upper_half = values[..., half_width:]
    return jnp.concatenate(
        [
            lower_half * cosine - upper_half * sine_part,
            upper_half * cosine + lower_half * sine_part,
        ],
        axis=-1,
    )


def shards(
    q_latent,
    new_latent,
    new_rope,
    cache_latent,
    cache_rope,
    lengths,
    assignment,
    w_uq,
    w_uk,
    w_uv,
    w_o,
):
    local_squares = (
        jnp.sum(w_uq * w_uq) + jnp.sum(w_uk * w_uk) + jnp.sum(w_uv * w_uv) + jnp.sum(w_o * w_o)
    )
    squares_total = over_axes(local_squares, DP_TP)
    weight_norm = jnp.sqrt(squares_total / (HEADS * (NOPE + ROPE) + 2 * HEADS * NOPE + D)).reshape(
        1
    )
    query_cast = w_uq.astype(jnp.bfloat16)
    key_cast = w_uk.astype(jnp.bfloat16)
    value_cast = w_uv.astype(jnp.bfloat16)
    mixed = (
        lax.all_to_all(query_cast, TP, split_axis=1, concat_axis=0, tiled=True),
        lax.all_to_all(key_cast, TP, split_axis=1, concat_axis=0, tiled=True),
        lax.all_to_all(value_cast, TP, split_axis=1, concat_axis=0, tiled=True),
    )
    query_up, key_up, value_up = gather_together((mixed[0], mixed[1], mixed[2]), DP, (0, 0, 0))
    out_cast = w_o.astype(jnp.bfloat16)
    seq_count = q_latent.shape[0]
    heads_here = key_up.shape[1] // NOPE
    selector = (assignment[0][:, None] == jnp.arange(seq_count, dtype=jnp.int32)[None, :]).astype(
        jnp.bfloat16
    )

    def to_slots(array):
        moved = jnp.dot(
            selector.T, array.reshape(seq_count, -1), preferred_element_type=jnp.float32
        )
        return moved.astype(jnp.bfloat16).reshape(array.shape)

    query_slots = to_slots(q_latent)
    latent_slots = to_slots(new_latent)
    rope_slots = to_slots(new_rope)
    projected = jnp.dot(
        query_slots.reshape(seq_count * NEWTOK, QRANK), query_up, preferred_element_type=jnp.float32
    )
    projected = projected.astype(jnp.bfloat16).reshape(seq_count, NEWTOK, heads_here, NOPE + ROPE)
    query_nope = projected[..., :NOPE]
    positions = lengths[:, None] + jnp.arange(NEWTOK, dtype=jnp.int32)[None, :]
    query_rot = rotate_half(widen(projected[..., NOPE:]), positions).astype(jnp.bfloat16)
    absorbed = jnp.einsum(
        "sqhn,chn->sqhc",
        query_nope,
        key_up.reshape(KVRANK, heads_here, NOPE),
        preferred_element_type=jnp.float32,
    ).astype(jnp.bfloat16)
    scale = (NOPE + ROPE) ** (-0.5)
    cache_scores = jnp.einsum(
        "sqhc,stc->sqht", absorbed, cache_latent, preferred_element_type=jnp.float32
    )
    cache_scores = (
        cache_scores
        + jnp.einsum("sqhr,srt->sqht", query_rot, cache_rope, preferred_element_type=jnp.float32)
    ) * scale
    valid = jnp.arange(CACHE, dtype=jnp.int32)[None, :] < lengths[:, None]
    cache_scores = jnp.where(valid[:, None, None, :], cache_scores, -jnp.inf)
    new_scores = jnp.einsum(
        "sqhc,skc->sqhk", absorbed, latent_slots, preferred_element_type=jnp.float32
    )
    new_scores = (
        new_scores
        + jnp.einsum("sqhr,skr->sqhk", query_rot, rope_slots, preferred_element_type=jnp.float32)
    ) * scale
    causal = jnp.arange(NEWTOK)[:, None] >= jnp.arange(NEWTOK)[None, :]
    new_scores = jnp.where(causal[None, :, None, :], new_scores, -jnp.inf)
    scores = jnp.concatenate([cache_scores, new_scores], axis=-1)
    largest = jnp.max(scores, axis=-1, keepdims=True)
    expo = jnp.exp(scores - largest)
    weights = (expo / jnp.sum(expo, axis=-1, keepdims=True)).astype(jnp.bfloat16)
    latent_out = jnp.einsum(
        "sqht,stc->sqhc", weights[..., :CACHE], cache_latent, preferred_element_type=jnp.float32
    )
    latent_out = (
        latent_out
        + jnp.einsum(
            "sqhk,skc->sqhc", weights[..., CACHE:], latent_slots, preferred_element_type=jnp.float32
        )
    ).astype(jnp.bfloat16)
    head_out = jnp.einsum(
        "sqhc,chv->sqhv",
        latent_out,
        value_up.reshape(KVRANK, heads_here, VDIM),
        preferred_element_type=jnp.float32,
    ).astype(jnp.bfloat16)
    request_out = jnp.dot(
        selector, head_out.reshape(seq_count, -1), preferred_element_type=jnp.float32
    )
    request_out = request_out.astype(jnp.bfloat16).reshape(seq_count * NEWTOK, heads_here * VDIM)
    out_rows = lax.all_to_all(out_cast, TP, split_axis=0, concat_axis=1, tiled=True)
    partial_out = jnp.dot(
        request_out,
        lax.all_gather(out_rows, DP, axis=1, tiled=True),
        preferred_element_type=jnp.float32,
    )
    reduced = lax.psum_scatter(partial_out, TP, scatter_dimension=1, tiled=True)
    attention_out = reduced.astype(jnp.bfloat16).reshape(seq_count, NEWTOK, -1)
    return (attention_out, weight_norm)


def solution(mesh):
    split = Mesh(mesh.devices.reshape(4, 4, 4, 2), ("dp_0", "dp_1", "tp_0", "tp_1"))
    placed = (
        P(DP, None, None),
        P(DP, None, None),
        P(DP, None, None),
        P(DP, None, None),
        P(DP, None, None),
        P(DP),
        P(DP, None),
        P(DP_TP, None),
        P(DP_TP, None),
        P(DP_TP, None),
        P(None, DP_TP),
    )
    return jax.shard_map(
        shards, mesh=split, in_specs=placed, out_specs=(P(DP, None, TP), P()), check_vma=False
    )
```

profile of v0, /device:TPU:1, one launch (start us, length us, event | category | flops | bytes accessed | tf_op | source)
XLA Modules:
  0.0 327.0 jit_solution(1335519092230340483)
XLA Ops:
  7.2 2.4 multiply_reduce_fusion.3
  9.6 5.8 %all-to-all-start.1 = ((bf16[4,8,1024]{2,0,1:T(4,128)(2,1)}), bf16[4,8,1024]{2,0,1:T(4,128)(2,1)S(1)}, u32[]{:S(2)}, u32[]{:S(2)}) async-start(bf16[4,8,1024]{2,0,1:T(4,128)(2,1)} %bitcast.2), calls=%async_computation.1 | async-start | bytes 131072 | tf_op jit(solution)/shard_map/all_to_all | solution.py:89
  15.4 2.2 multiply_reduce_fusion.2
  17.6 2.6 all-to-all-done.1
  20.2 4.0 %all-to-all-start.2 = ((bf16[4,8,1024]{2,0,1:T(4,128)(2,1)}), bf16[4,8,1024]{2,0,1:T(4,128)(2,1)S(1)}, u32[]{:S(2)}, u32[]{:S(2)}) async-start(bf16[4,8,1024]{2,0,1:T(4,128)(2,1)} %bitcast.4), calls=%async_computation.2 | async-start | bytes 131072 | tf_op jit(solution)/shard_map/all_to_all | solution.py:90
  24.2 2.3 multiply_reduce_fusion.1
  26.7 0.8 copy.47
  27.5 1.6 all-to-all-done.2
  29.1 4.1 %all-to-all-start = ((bf16[12,8,1536]{2,0,1:T(8,128)(2,1)}), bf16[12,8,1536]{2,0,1:T(8,128)(2,1)S(1)}, u32[]{:S(2)}, u32[]{:S(2)}) async-start(bf16[12,8,1536]{2,0,1:T(8,128)(2,1)} %copy.47), calls=%async_computation | async-start | bytes 786432 | tf_op jit(solution)/shard_map/all_to_all | solution.py:88
  33.9 7.1 %all-to-all-done = bf16[12,8,1536]{2,0,1:T(8,128)(2,1)S(1)} async-done(((bf16[12,8,1536]{2,0,1:T(8,128)(2,1)}), bf16[12,8,1536]{2,0,1:T(8,128)(2,1)S(1)}, u32[]{:S(2)}, u32[]{:S(2)}) %all-to-all-start) | async-done | bytes 294944 | tf_op jit(solution)/shard_map/all_to_all | solution.py:88
  41.0 1.1 reshape.130
  42.1 1.9 pad_maximum_fusion.1
  44.0 1.1 multiply_reduce_fusion
  45.2 18.0 %all_to_all.67 = bf16[8,1024,56]{1,2,0:T(8,128)(2,1)} all-to-all(bf16[8,1024,56]{1,2,0:T(8,128)(2,1)S(1)} %bitcast.73), channel_id=1, replica_groups=mesh['dp_0'=4,'dp_1'=4,'tp_0'=4,'tp_1'=2] {'tp_0','tp_1'}, dimensions={0} | all-to-all | bytes 1835008 | tf_op jit(solution)/shard_map/all_to_all | solution.py:164
  64.8 1.1 reshape_reshape.6
  65.9 1.2 copy.84
  67.5 1.2 reshape.147
  69.1 0.8 copy.68
  70.1 2.9 multiply_cosine_fusion
  72.9 35.9 %all-gather.6.cloned.1.call-done = bf16[3407872]{0:T(1024)(128)(2,1)} async-done(((bf16[212992]{0:T(1024)(128)(2,1)}), bf16[3407872]{0:T(1024)(128)(2,1)}) %all-gather.6.cloned.1.call-update) | async-done | bytes 6815760 | tf_op jit(solution)/shard_map/all_gather | solution.py:35
  108.8 6.5 %reshape.143 = bf16[16,212992]{1,0:T(8,128)(2,1)} reshape(bf16[3407872]{0:T(1024)(128)(2,1)} %all-gather.6.cloned.1.call-done) | data formatting | bytes 13631488 | tf_op jit(solution)/shard_map/all_gather | solution.py:35
  115.4 4.0 %slice.38 = bf16[16,147456]{1,0:T(8,128)(2,1)} slice(bf16[16,212992]{1,0:T(8,128)(2,1)} %reshape.143), slice={[0:16], [0:147456]} | slice | bytes 9437184 | tf_op jit(solution)/shard_map/slice | solution.py:37
  119.4 5.5 %reshape_reshape.7 = bf16[1536,1536]{1,0:T(8,128)(2,1)} reshape(bf16[16,147456]{1,0:T(8,128)(2,1)} %slice.38) | data formatting | bytes 9437184 | tf_op jit(solution)/shard_map/reshape;reshape | solution.py:30
  124.9 6.0 %convolution_convert_fusion.2 = bf16[512,1536]{1,0:T(8,128)(2,1)} fusion(bf16[512,1536]{1,0:T(8,128)(2,1)S(1)} %reshape_reshape.6, bf16[1536,1536]{1,0:T(8,128)(2,1)} %reshape_reshape.7), kind=kOutput, calls=%fused_computation.17 | convolution fusion | flops 2416705536 | bytes 7864320 | tf_op jit(solution)/shard_map/dot_general | solution.py:109
  131.0 3.3 %reshape.134 = bf16[128,4,8,192]{3,2,1,0:T(8,128)(2,1)S(1)} reshape(bf16[512,1536]{1,0:T(8,128)(2,1)} %convolution_convert_fusion.2) | data formatting | bytes 3145728 | tf_op jit(solution)/shard_map/reshape | solution.py:112
  134.5 3.7 %fusion.34 = (bf16[16,32768]{1,0:T(8,128)(2,1)}, bf16[16,32768]{1,0:T(8,128)(2,1)}) fusion(bf16[16,212992]{1,0:T(8,128)(2,1)} %reshape.143), kind=kLoop, calls=%fused_computation.54 | loop fusion | bytes 4194304 | tf_op jit(solution)/shard_map/slice | solution.py:37
  138.2 1.6 reshape_reshape_reshape.7
  139.8 3.4 %convert_bitcast_fusion = bf16[128,4,8,512]{0,3,1,2:T(8,128)(2,1)} fusion(bf16[128,4,8,128]{3,2,1,0:T(8,128)(2,1)S(1)} %slice.39, bf16[512,8,128,1]{2,1,0,3:T(8,128)(2,1)S(1)} %bitcast.71), kind=kOutput, calls=%fused_computation.16 | convolution fusion | flops 538968064 | bytes 6291456 | tf_op jit(solution)/shard_map/sqhn,chn->sqhc/dot_general | solution.py:116
  143.2 8.2 %copy.52 = bf16[128,4,8,512]{3,2,1,0:T(8,128)(2,1)} copy(bf16[128,4,8,512]{0,3,1,2:T(8,128)(2,1)} %convert_bitcast_fusion) | data formatting | bytes 8388608 | tf_op jit(solution)/shard_map/convert_element_type | solution.py:121
  151.7 2.5 reshape_reshape_reshape.6
  154.2 1.9 subtract_convert_fusion
  156.6 1.2 fusion.24
  157.8 1.6 fusion.36
  159.4 18.4 %fusion.2 = f32[128,4,8,256]{3,2,1,0:T(8,128)} fusion(bf16[128,4,8,512]{3,2,1,0:T(8,128)(2,1)} %copy.52, bf16[128,256,512]{2,1,0:T(8,128)(2,1)} %param.14), kind=kOutput, calls=%fused_computation.2 | convolution fusion | flops 1073741824 | bytes 41943040 | tf_op jit(solution)/shard_map/sqhc,stc->sqht/dot_general | solution.py:123
  177.7 5.7 %fusion.35 = (f32[128,4,8]{2,1,0:T(4,128)S(1)}, f32[128,4,8,256]{3,2,1,0:T(8,128)S(1)}) fusion(f32[128,4,8,256]{3,2,1,0:T(8,128)} %fusion.2, bf16[128,64,256]{2,1,0:T(8,128)(2,1)} %param.15, bf16[128,4,8,32]{3,2,1,0:T(8,128)(2,1)} %copy-done.3, bf16[128,4,8,32]{3,2,1,0:T(8,128)(2,1)S(1)} %get-tuple-element.4, pred[128,256]{1,0:T(8,128)(4,1)S(1)} %iota_compare_fusion), kind=kOutput, calls=%fused_computation.55 | convolution fusion | flops 139456512 | bytes 13156352 | tf_op jit(solution)/shard_map/sqhr,srt->sqht/dot_general | solution.py:128
  183.5 1.7 fusion.5
  185.2 3.4 %divide_convert_fusion = bf16[128,4,8,260]{3,2,1,0:T(8,128)(2,1)} fusion(f32[128,4,8,4]{3,2,1,0:T(8,128)S(1)} %get-tuple-element.19, f32[128,4,8,256]{3,2,1,0:T(8,128)S(1)} %get-tuple-element.17, f32[128,4,8]{2,1,0:T(4,128)S(1)} %fusion.5, f32[128,4,8]{2,1,0:T(4,128)S(1)} %reduce_max.22), kind=kLoop, calls=%fused_computation.8 | loop fusion | flops 4259840 | bytes 6422528 | tf_op jit(solution)/shard_map/convert_element_type | solution.py:144
  188.6 20.5 %fusion = f32[128,4,8,512]{3,2,1,0:T(8,128)} fusion(bf16[128,256,512]{2,1,0:T(8,128)(2,1)} %param.14, bf16[128,4,8,260]{3,2,1,0:T(8,128)(2,1)} %divide_convert_fusion), kind=kOutput, calls=%fused_computation | convolution fusion | flops 1073741824 | bytes 44040192 | tf_op jit(solution)/shard_map/sqht,stc->sqhc/dot_general | solution.py:145
  209.1 5.0 %add_convert_fusion = bf16[128,4,8,512]{3,2,1,0:T(8,128)(2,1)S(1)} fusion(f32[128,4,8,512]{3,2,1,0:T(8,128)} %fusion, bf16[128,4,8,260]{3,2,1,0:T(8,128)(2,1)} %divide_convert_fusion, bf16[128,4,512,1]{2,1,0,3:T(4,128)(2,1)S(1)} %copy-done.6), kind=kOutput, calls=%fused_computation.4 | convolution fusion | flops 20971520 | bytes 14155776 | tf_op jit(solution)/shard_map/sqhk,skc->sqhc/dot_general | solution.py:150
  214.1 4.9 %fusion.16 = bf16[128,4,8,128]{0,3,1,2:T(8,128)(2,1)S(1)} fusion(bf16[128,4,8,512]{3,2,1,0:T(8,128)(2,1)S(1)} %add_convert_fusion, bf16[512,8,128,1]{2,1,0,3:T(8,128)(2,1)S(1)} %bitcast.80), kind=kOutput, calls=%fused_computation.25 | convolution fusion | flops 537395200 | bytes 6291456 | tf_op jit(solution)/shard_map/sqhc,chv->sqhv/dot_general | solution.py:154
  220.3 14.3 %fusion.37 = f32[512,7168]{1,0:T(8,128)} fusion(bf16[512,1024]{1,0:T(8,128)(2,1)S(1)} %reshape.140, bf16[1024,7168]{0,1:T(8,128)(2,1)} %all-gather.4.cloned.1.call-done), kind=kOutput, calls=%fused_computation.57 | convolution fusion | flops 7516192768 | bytes 30408704 | tf_op jit(solution)/shard_map/dot_general | solution.py:165
  237.2 9.0 %psum.28 = f32[]{:T(128)} all-reduce(f32[]{:T(128)S(6)} %add.57), channel_id=1, replica_groups=mesh['dp_0'=4,'dp_1'=4,'tp_0'=4,'tp_1'=2] {'dp_0'}, use_global_device_ids=true, to_apply=%region_8.9 | all-reduce | flops 1 | bytes 8 | tf_op jit(solution)/shard_map/psum | solution.py:23
  246.2 8.0 %psum.29 = f32[]{:T(128)} all-reduce(f32[]{:T(128)} %psum.28), channel_id=1, replica_groups=mesh['dp_0'=4,'dp_1'=4,'tp_0'=4,'tp_1'=2] {'dp_1'}, use_global_device_ids=true, to_apply=%region_9.10 | all-reduce | flops 1 | bytes 8 | tf_op jit(solution)/shard_map/psum | solution.py:23
  254.3 8.8 %psum.30 = f32[]{:T(128)} all-reduce(f32[]{:T(128)} %psum.29), channel_id=1, replica_groups=mesh['dp_0'=4,'dp_1'=4,'tp_0'=4,'tp_1'=2] {'tp_0'}, use_global_device_ids=true, to_apply=%region_10.11 | all-reduce | flops 1 | bytes 8 | tf_op jit(solution)/shard_map/psum | solution.py:23
  263.1 9.0 %psum.31 = f32[]{:T(128)} all-reduce(f32[]{:T(128)} %psum.30), channel_id=1, replica_groups=mesh['dp_0'=4,'dp_1'=4,'tp_0'=4,'tp_1'=2] {'tp_1'}, use_global_device_ids=true, to_apply=%region_11.12 | all-reduce | flops 1 | bytes 8 | tf_op jit(solution)/shard_map/psum | solution.py:23
  272.8 43.5 %reduce-scatter.2.cloned.1.call-done = f32[512,896]{1,0:T(8,128)} async-done(((f32[512,7168]{1,0:T(8,128)}), f32[512,896]{1,0:T(8,128)}) %reduce-scatter.2.cloned.1.call-update) | async-done | bytes 1835024 | tf_op jit(solution)/shard_map/reduce_scatter | solution.py:170
  316.3 1.6 convert_element_type.77
  317.9 1.1 reshape.141
  (55 shorter events, 5.8 us)
Async XLA Ops:
  7.2 61.5 %copy-start = (bf16[128,4,64]{0,2,1:T(8,128)(2,1)S(1)}, bf16[128,4,64]{0,2,1:T(8,128)(2,1)}, u32[]{:S(2)}) copy-start(bf16[128,4,64]{0,2,1:T(8,128)(2,1)} %param.13) | copy-start | bytes 196612
  7.2 36.9 %copy-start.7 = (f32[8192,56]{0,1:T(8,128)S(1)}, f32[8192,56]{0,1:T(8,128)}, u32[]{:S(2)}) copy-start(f32[8192,56]{0,1:T(8,128)} %param.21) | copy-start | bytes 5505028
  9.6 10.6 %all-to-all-start.1 = ((bf16[4,8,1024]{2,0,1:T(4,128)(2,1)}), bf16[4,8,1024]{2,0,1:T(4,128)(2,1)S(1)}, u32[]{:S(2)}, u32[]{:S(2)}) async-start(bf16[4,8,1024]{2,0,1:T(4,128)(2,1)} %bitcast.2), calls=%async_computation.1 | async-start | bytes 131072 | tf_op jit(solution)/shard_map/all_to_all | solution.py:89
  20.2 8.9 %all-to-all-start.2 = ((bf16[4,8,1024]{2,0,1:T(4,128)(2,1)}), bf16[4,8,1024]{2,0,1:T(4,128)(2,1)S(1)}, u32[]{:S(2)}, u32[]{:S(2)}) async-start(bf16[4,8,1024]{2,0,1:T(4,128)(2,1)} %bitcast.4), calls=%async_computation.2 | async-start | bytes 131072 | tf_op jit(solution)/shard_map/all_to_all | solution.py:90
  29.1 11.9 %all-to-all-start = ((bf16[12,8,1536]{2,0,1:T(8,128)(2,1)}), bf16[12,8,1536]{2,0,1:T(8,128)(2,1)S(1)}, u32[]{:S(2)}, u32[]{:S(2)}) async-start(bf16[12,8,1536]{2,0,1:T(8,128)(2,1)} %copy.47), calls=%async_computation | async-start | bytes 786432 | tf_op jit(solution)/shard_map/all_to_all | solution.py:88
  33.3 75.6 %all-gather.6.cloned.1.call-start = ((), (), s32[]{:S(2)}) async-start(), calls=%async_computation.7 | async-start | bytes 7241728 | tf_op jit(solution)/shard_map/all_gather | solution.py:35
  42.1 21.8 %copy-start.8 = (bf16[128,4,1536]{2,1,0:T(4,128)(2,1)S(1)}, bf16[128,4,1536]{2,1,0:T(4,128)(2,1)}, u32[]{:S(2)}) copy-start(bf16[128,4,1536]{2,1,0:T(4,128)(2,1)} %param.11) | copy-start | bytes 4718596
  44.0 176.3 %all-gather.4.cloned.1.call-start = ((), (), s32[]{:S(2)}) async-start(), calls=%async_computation.5 | async-start | bytes 15597568 | tf_op jit(solution)/shard_map/all_gather | solution.py:167
  45.1 19.0 %copy-start.11 = (s32[1,128]{1,0:T(1,128)S(1)}, s32[1,128]{1,0:T(1,128)}, u32[]{:S(2)}) copy-start(s32[1,128]{1,0:T(1,128)} %param.17) | copy-start | bytes 1540
  63.2 253.1 %reduce-scatter.2.cloned.1.call-start = ((), (), s32[]{:S(2)}) async-start(), calls=%async_computation.6 | async-start | bytes 16515072 | tf_op jit(solution)/shard_map/reduce_scatter | solution.py:170
  64.1 5.7 %copy-start.12 = (s32[128]{0:T(128)S(1)}, s32[128]{0:T(128)}, u32[]{:S(2)}) copy-start(s32[128]{0:T(128)} %param.16) | copy-start | bytes 1540
  134.3 3.9 %copy-start.4 = (bf16[128,4,8,192]{3,2,1,0:T(8,128)(2,1)}, bf16[128,4,8,192]{3,2,1,0:T(8,128)(2,1)S(1)}, u32[]{:S(2)}) copy-start(bf16[128,4,8,192]{3,2,1,0:T(8,128)(2,1)S(1)} %reshape.134) | copy-start | bytes 4718596
  143.2 8.2 %slice-start = ((bf16[128,4,8,192]{3,2,1,0:T(8,128)(2,1)}), bf16[128,4,8,64]{3,2,1,0:T(8,128)(2,1)S(1)}, s32[]{:S(2)}) async-start(bf16[128,4,8,192]{3,2,1,0:T(8,128)(2,1)} %copy-done.4), calls=%async_computation.8 | async-start | bytes 2097152 | tf_op jit(solution)/shard_map/slice | solution.py:115
  154.2 2.3 copy-start.2
  154.2 2.4 copy-start.5
  156.6 1.2 copy-start.3
  156.6 1.2 copy-start.10
  188.6 20.5 %copy-start.6 = (bf16[128,4,512,1]{2,1,0,3:T(4,128)(2,1)S(1)}, bf16[128,4,512,1]{2,1,0,3:T(4,128)(2,1)}, u32[]{:S(2)}) copy-start(bf16[128,4,512,1]{2,1,0,3:T(4,128)(2,1)} %reshape.147) | copy-start | bytes 1572868
  209.1 5.0 %copy-start.9 = (bf16[512,8,128]{2,1,0:T(8,128)(2,1)S(1)}, bf16[512,8,128]{2,1,0:T(8,128)(2,1)}, u32[]{:S(2)}) copy-start(bf16[512,8,128]{2,1,0:T(8,128)(2,1)} %reshape_reshape_reshape.6) | copy-start | bytes 3145732
  234.7 84.4 %copy-start.1 = (bf16[128,4,64]{0,2,1:T(8,128)(2,1)S(1)}, bf16[128,4,64]{0,2,1:T(8,128)(2,1)}, u32[]{:S(2)}) copy-start(bf16[128,4,64]{0,2,1:T(8,128)(2,1)} %param.13) | copy-start | bytes 196612
Sparse Core Ops, SparseCore 0:
  44.1 64.6 all-gather.5
  111.0 100.1 all-gather.3
  234.8 81.5 reduce-scatter.1
where the time goes:
time: 330 us; the launch traced here: 327 us
  waiting for transfers between devices  90.8 us (28%)
  matrix products  82.8 us (25%)
  blocking collectives  52.9 us (16%)
  local copies, waits for them, and re-layouts  45.3 us (14%)
  other arithmetic  21.8 us (7%)
  between operations  18.7 us (6%)
  starting transfers between devices  14.6 us (4%)
    reduce_scatter x1, waiting for transfers between devices, shards(): reduced = lax.psum_scatter(partial_out, TP, scatter_dimension=1, tiled=True)  43.5 us
    all_gather x1, waiting for transfers between devices, gather_together(): lines, at, finished = (lax.all_gather(ravelled, axis), 0, [])  35.9 us
    psum x4, blocking collectives, over_axes(): value = lax.psum(value, axis)  34.9 us
    dot_general x1, matrix products, shards(): jnp.einsum('sqht,stc->sqhc', weights[..., :CACHE], cache_latent, preferre...  20.5 us
    dot_general x1, matrix products, shards(): jnp.einsum('sqhc,stc->sqht', absorbed, cache_latent, preferred_element_ty...  18.4 us
    all_to_all x1, blocking collectives, shards(): lax.all_to_all(out_cast, TP, split_axis=0, concat_axis=1, tiled=True)  18 us
    dot_general x1, matrix products, shards(): jnp.dot(request_out, lax.all_gather(out_rows, DP, axis=1, tiled=True), pr...  14.3 us
    convert_element_type x1, local copies, waits for them, and re-layouts, shards(): absorbed = jnp.einsum('sqhn,chn->sqhc', query_nope, key_up.reshape(KVRANK...  8.21 us
  transfers between devices with their start and end apart: 6, of which 5 were waited for; matrix products, arithmetic and copies ran while one was open for 39% of the time, Pallas kernels for 0%

commit v1 on v0

v1 whole, which is shorter than its diff:
```python
import jax
import jax.numpy as jnp
from jax import lax
from jax.experimental import pallas as pl
from jax.experimental.pallas import tpu as pltpu
from jax.sharding import Mesh
from jax.sharding import PartitionSpec as P

D = 7168
QRANK = 1536
KVRANK = 512
NOPE = 128
ROPE = 64
VDIM = 128
HEADS = 64
NEWTOK = 4
CACHE = 256
SEQS = 128
TOK = SEQS * NEWTOK
HL = 8
GROUPS = SEQS // 4
SLOTS = 4
BF = jnp.bfloat16
F32 = jnp.float32
DP_TP = ("dp_0", "dp_1", "tp_0", "tp_1")
TP = ("tp_0", "tp_1")
DP = ("dp_0", "dp_1")
SCALE = (NOPE + ROPE) ** (-0.5)


def nt(a, b):
    return lax.dot_general(a, b, (((1,), (1,)), ((), ())), preferred_element_type=F32)


def nn(a, b):
    return lax.dot_general(a, b, (((1,), (0,)), ((), ())), preferred_element_type=F32)


def project(q_ref, u_ref, cos_ref, sin_ref, abs_ref, qr_ref):
    def nope_pair(i, carry):
        cols = pl.ds(pl.multiple_of(i * 256, 256), 256)
        both = nn(q_ref[...], u_ref[:, :, 0:96, cols].reshape(QRANK, 256)).astype(BF)
        for j in range(2):
            own_cols = pl.ds(pl.multiple_of(i * 256 + j * 128, 128), 128)
            keys = u_ref[:, :, 96:128, own_cols].reshape(KVRANK, 128)
            abs_ref[i * 2 + j] = nt(both[:, j * 128 : (j + 1) * 128], keys).astype(BF)
        return carry

    lax.fori_loop(0, 4, nope_pair, 0)
    lane = lax.broadcasted_iota(jnp.int32, (TOK, 128), 1)
    row = lax.broadcasted_iota(jnp.int32, (TOK, 128), 0)
    own = lax.rem(row // 4, 4)
    low = lax.rem(lane, 64) < 32

    def pe_quad(i, carry):
        cols = pl.ds(pl.multiple_of(1024 + i * 256, 256), 256)
        four = nn(q_ref[...], u_ref[:, :, 0:96, cols].reshape(QRANK, 256)).astype(BF).astype(F32)
        for j in range(2):
            pe = four[:, j * 128 : (j + 1) * 128]
            other = jnp.where(low, pltpu.roll(pe, 96, 1), pltpu.roll(pe, 32, 1))
            rot = pe * cos_ref[...] + other * sin_ref[...]
            flip = pltpu.roll(rot, 64, 1)
            for odd in range(2):
                twice = jnp.where((lane < 64) == (odd == 0), rot, flip)
                head = i * 4 + j * 2 + odd
                for half in range(2):
                    kept = jnp.where(own == 2 * half + lane // 64, twice, 0.0)
                    qr_ref[head, :, half * 128 : (half + 1) * 128] = kept.astype(BF)
        return carry

    lax.fori_loop(0, 2, pe_quad, 0)


def scores_of(g, abs_ref, qr_ref, latn_ref, ropn_ref, lat, rop, sc_ref, scn_ref):
    rows = pl.ds(pl.multiple_of(g * 16, 16), 16)
    q = abs_ref[:, rows, :].reshape(128, KVRANK)
    qr = qr_ref[:, rows, :].reshape(128, 256)
    seq = lax.rem(lax.broadcasted_iota(jnp.int32, (128, KVRANK), 0) // 4, 4)
    zero = jnp.zeros_like(q)
    parts = jnp.concatenate([jnp.where(seq == s, q, zero) for s in range(4)], axis=1)
    keys = jnp.concatenate([lat[s] for s in range(4)], axis=1)
    sc_ref[...] = nt(parts, keys) + nn(qr, rop[...].reshape(256, CACHE))
    scn_ref[...] = nt(q, latn_ref[rows, :]) + nt(qr, ropn_ref[rows, :])


def attend(g, len_ref, latn_ref, lat, sc_ref, scn_ref, lo_ref):
    row = lax.broadcasted_iota(jnp.int32, (128, CACHE), 0)
    seq = lax.rem(row // 4, 4)
    limit = jnp.where(
        seq == 0,
        len_ref[g * 4],
        jnp.where(
            seq == 1, len_ref[g * 4 + 1], jnp.where(seq == 2, len_ref[g * 4 + 2], len_ref[g * 4 + 3])
        ),
    )
    at = lax.broadcasted_iota(jnp.int32, (128, CACHE), 1)
    sc = jnp.where(at < limit, sc_ref[...] * SCALE, -jnp.inf)
    nrow = lax.broadcasted_iota(jnp.int32, (128, 16), 0)
    ncol = lax.broadcasted_iota(jnp.int32, (128, 16), 1)
    fits = (lax.rem(nrow // 4, 4) == ncol // 4) & (lax.rem(ncol, 4) <= lax.rem(nrow, 4))
    scn = jnp.where(fits, scn_ref[...] * SCALE, -jnp.inf)
    top = jnp.maximum(
        jnp.max(sc, axis=1, keepdims=True), jnp.max(scn, axis=1, keepdims=True)
    )
    ex = jnp.exp(sc - top)
    exn = jnp.exp(scn - top)
    total = jnp.sum(ex, axis=1, keepdims=True) + jnp.sum(exn, axis=1, keepdims=True)
    share = 1.0 / total
    w = (ex * share).astype(BF)
    wn = (exn * share).astype(BF)
    zero = jnp.zeros_like(w)
    parts = jnp.concatenate([jnp.where(seq == s, w, zero) for s in range(4)], axis=1)
    rows = pl.ds(pl.multiple_of(g * 16, 16), 16)
    out = nn(parts, lat[...].reshape(4 * CACHE, KVRANK)) + nn(wn, latn_ref[rows, :])
    lo_ref[:, rows, :] = out.astype(BF).reshape(HL, 16, KVRANK)


MESH = pl.DeviceIdType.MESH
CHUNKS = 4
HALF = 64


def around(i, d):
    return lax.rem(i + d + 4, 4)


def layer_kernel(
    uq_ref, wk_ref, wv_ref, wo_ref, q_ref, latk_ref, ropk_ref, selk_ref, sel_ref, cos_ref, sin_ref,
    len_ref, lat_hbm, rop_hbm,
    out_ref, norm_ref,
    stage, packs, rp, opack, orp, u_ref, wo_all, nsend, ntp, ny, nz,
    qs_ref, latn_ref, ropn_ref, abs_ref, qr_ref, lo_ref, lat_ref, rop_ref, sc0, scn0, sc1, scn1,
    ho_ref, hb_ref, ct_ref, r1_ref, rx_ref, fs_ref, ft_ref, ot_ref,
    lat_sem, rop_sem, a2a_s, a2a_r, o2a_s, o2a_r, nt_s, nt_r, nyz_s, nyz_r, ag_s, ag_r,
    oz_s, oz_r, od_s, od_r, d2_s, d2_r, hy_s, hy_r, r1_s, r1_r, r2_s, r2_r, f_s, f_r,
):
    z, y = lax.axis_index("dp_0"), lax.axis_index("dp_1")
    x, c = lax.axis_index("tp_0"), lax.axis_index("tp_1")
    t = x * 2 + c
    sends = []

    def copy_to(src, dst, ss, rs, **axes):
        names = {"z": "dp_0", "y": "dp_1", "x": "tp_0", "c": "tp_1"}
        return pltpu.make_async_remote_copy(
            src_ref=src, dst_ref=dst, send_sem=ss, recv_sem=rs,
            device_id={names[n]: v for n, v in axes.items()}, device_id_type=MESH,
        )

    def send(src, dst, ss, rs, **axes):
        made = copy_to(src, dst, ss, rs, **axes)
        made.start()
        sends.append(made)

    def arrived(dst, ss, rs):
        copy_to(dst, dst, ss, rs, c=1 - c).wait_recv()

    barrier = pltpu.get_barrier_semaphore()

    def greet(**axes):
        names = {"z": "dp_0", "y": "dp_1", "x": "tp_0", "c": "tp_1"}
        pl.semaphore_signal(
            barrier, inc=1, device_id={names[n]: v for n, v in axes.items()}, device_id_type=MESH
        )

    for dt in range(1, 8):
        peer = lax.rem(t + dt, 8)
        greet(x=peer // 2, c=lax.rem(peer, 2))
    for d in range(1, 4):
        greet(z=around(z, d))
        greet(y=around(y, d))
        greet(y=around(y, d), c=1 - c)

    def fetch(g):
        slot = lax.rem(g, SLOTS)
        return (
            pltpu.make_async_copy(lat_hbm.at[pl.ds(g * 4, 4)], lat_ref.at[slot], lat_sem.at[slot]),
            pltpu.make_async_copy(rop_hbm.at[pl.ds(g * 4, 4)], rop_ref.at[slot], rop_sem.at[slot]),
        )

    def start(g):
        for made in fetch(g):
            made.start()

    def wait(g):
        for made in fetch(g):
            made.wait()

    for g in range(SLOTS - 1):
        start(g)

    lane12 = lax.broadcasted_iota(jnp.int32, (12, 128), 1)

    def fold(v):
        rows, cols = v.shape
        total = jnp.zeros((8, 128), F32)
        for i in range(rows // 8):
            for j in range(cols // 128):
                part = v[i * 8 : i * 8 + 8, j * 128 : j * 128 + 128]
                total = total + part * part
        return total

    def pack_one(p, squares):
        for i in range(4):
            v = uq_ref[:, pl.ds(pl.multiple_of(p * 1536 + i * 384, 128), 384)]
            v0, v1, v2 = v[:, 0:128], v[:, 128:256], v[:, 256:384]
            stage[p, 0:12, i * 256 : i * 256 + 128] = v0
            stage[p, 0:12, i * 256 + 128 : i * 256 + 256] = pltpu.roll(
                jnp.where(lane12 < 64, v2, v1), 64, 1
            )
            stage[p, 0:12, 1024 + i * 128 : 1152 + i * 128] = jnp.where(lane12 < 64, v1, v2)
            stage[p, i * 4 : i * 4 + 4, 1536:1792] = wv_ref[
                :, pl.ds(pl.multiple_of(p * 1024 + i * 256, 128), 256)
            ]
        stage[p, 12:16, 0:1024] = wk_ref[:, pl.ds(pl.multiple_of(p * 1024, 128), 1024)]
        stage[p, 12:16, 1024:1536] = jnp.zeros((4, 512), F32)
        whole = stage[p]
        packs[p] = whole.astype(BF)
        return squares + fold(whole)

    squares = lax.fori_loop(0, 8, pack_one, jnp.zeros((8, 128), F32))
    pl.semaphore_wait(barrier, 16)
    for dt in range(1, 8):
        peer = lax.rem(t + dt, 8)
        send(packs.at[peer], rp.at[t], a2a_s.at[dt], a2a_r.at[dt], x=peer // 2, c=lax.rem(peer, 2))
    rp[t] = packs[t]

    def pack_out(p, squares):
        v = wo_ref[:, pl.ds(pl.multiple_of(p * 1024, 128), 1024)]
        opack[p] = v.astype(BF)
        return squares + fold(v)

    squares = lax.fori_loop(0, 8, pack_out, squares)
    nsend[0] = squares
    ntp[t] = squares
    for dt in range(1, 8):
        peer = lax.rem(t + dt, 8)
        where = dict(x=peer // 2, c=lax.rem(peer, 2))
        send(nsend.at[0], ntp.at[t], nt_s.at[dt], nt_r.at[dt], **where)
        send(opack.at[peer], orp.at[t], o2a_s.at[dt], o2a_r.at[dt], **where)
    orp[t] = opack[t]

    for dt in range(1, 8):
        arrived(rp.at[lax.rem(t + 8 - dt, 8)], a2a_s.at[dt], a2a_r.at[dt])
    big = rp[...].reshape(128, 1792)
    r = lax.broadcasted_iota(jnp.int32, (128, 128), 0)
    col = lax.broadcasted_iota(jnp.int32, (128, 128), 1)
    origin = jnp.where(
        r < 96, (r // 12) * 16 + lax.rem(r, 12), ((r - 96) // 4) * 16 + 12 + lax.rem(r - 96, 4)
    )
    order = jnp.where(col == origin, 1.0, 0.0).astype(BF)
    sorted_rows = nn(order, big[:, 0:1536]).astype(BF)
    r32 = lax.broadcasted_iota(jnp.int32, (32, 128), 0)
    col32 = lax.broadcasted_iota(jnp.int32, (32, 128), 1)
    uv_parts = []
    for i in range(4):
        pick = jnp.where(col32 == (r32 // 4) * 16 + i * 4 + lax.rem(r32, 4), 1.0, 0.0).astype(BF)
        uv_parts.append(nn(pick, big[:, 1536:1792]).astype(BF))
    own_uv = jnp.concatenate(uv_parts, axis=1)
    u_ref[z, y, 0:96, 0:1536] = sorted_rows[0:96]
    u_ref[z, y, 96:128, 0:1024] = sorted_rows[96:128, 0:1024]
    u_ref[z, y, 96:128, 1024:1664] = own_uv[:, 0:640]
    for i in range(3):
        u_ref[z, y, i * 32 : i * 32 + 32, 1536:1664] = own_uv[:, 640 + i * 128 : 768 + i * 128]

    def piece(half, ia, ib, sub=None):
        rows = pl.ds(half * 64, 64) if sub is None else pl.ds(half * 64 + sub * 32, 32)
        return u_ref.at[ib, ia, rows] if half == 0 else u_ref.at[ia, ib, rows]

    def step(half, along_first, to):
        first, second = ("y", "z") if half == 0 else ("z", "y")
        return {first if along_first else second: to}

    where_a = [y, z]
    where_b = [z, y]

    def sems(half, n):
        return ag_s.at[half * 20 + n], ag_r.at[half * 20 + n]

    offsets = (0, -1, 1, 2)

    def second_send(half, p):
        a, b = where_a[half], where_b[half]
        ia = around(a, offsets[p])
        for k, d in enumerate((1, -1)):
            ref = piece(half, ia, b)
            send(ref, ref, *sems(half, 4 + p * 2 + k), **step(half, False, around(b, d)))

    def second_forward(half, p):
        a, b = where_a[half], where_b[half]
        ia = around(a, offsets[p])
        for k, d in enumerate((1, -1)):
            arrived(piece(half, ia, around(b, -d)), *sems(half, 4 + p * 2 + k))
            ref = piece(half, ia, around(b, -d), k)
            send(ref, ref, *sems(half, 12 + p * 2 + k), **step(half, False, around(b, d)))

    for half in range(2):
        a, b = where_a[half], where_b[half]
        for k, d in enumerate((1, -1)):
            ref = piece(half, a, b)
            send(ref, ref, *sems(half, k), **step(half, True, around(a, d)))
    for half in range(2):
        second_send(half, 0)

    qs_ref[...] = nn(selk_ref[...], q_ref[...]).astype(BF)
    latn_ref[...] = nn(selk_ref[...], latk_ref[...]).astype(BF)
    rope_rows = jnp.concatenate([ropk_ref[k] for k in range(4)], axis=1)
    ropn_ref[...] = nt(selk_ref[...], jnp.concatenate([rope_rows] * 4, axis=0)).astype(BF)

    for dt in range(1, 8):
        arrived(ntp.at[lax.rem(t + 8 - dt, 8)], nt_s.at[dt], nt_r.at[dt])
    line = ntp[0]
    for i in range(1, 8):
        line = line + ntp[i]
    nsend[1] = line
    ny[y] = line
    for d in range(1, 4):
        send(nsend.at[1], ny.at[y], nyz_s.at[0, d], nyz_r.at[0, d], y=around(y, d))

    for half in range(2):
        a, b = where_a[half], where_b[half]
        for k, d in enumerate((1, -1)):
            arrived(piece(half, around(a, -d), b), *sems(half, k))
            ref = piece(half, around(a, -d), b, k)
            send(ref, ref, *sems(half, 2 + k), **step(half, True, around(a, d)))
    for half in range(2):
        second_send(half, 1)
        second_send(half, 2)
    for half in range(2):
        second_forward(half, 0)
    for d in range(1, 4):
        arrived(ny.at[around(y, -d)], nyz_s.at[0, d], nyz_r.at[0, d])
    plane = ((ny[0] + ny[1]) + ny[2]) + ny[3]
    nsend[2] = plane
    nz[z] = plane
    for d in range(1, 4):
        send(nsend.at[2], nz.at[z], nyz_s.at[1, d], nyz_r.at[1, d], z=around(z, d))
    for half in range(2):
        a, b = where_a[half], where_b[half]
        for k in range(2):
            arrived(piece(half, around(a, 2), b, k), *sems(half, 2 + k))
        second_send(half, 3)
    for p in range(1, 3):
        for half in range(2):
            second_forward(half, p)

    for dt in range(1, 8):
        arrived(orp.at[lax.rem(t + 8 - dt, 8)], o2a_s.at[dt], o2a_r.at[dt])
    wo_all[c, z] = jnp.concatenate([orp[i].astype(F32) for i in range(8)], axis=0).astype(BF)
    for half in range(2):
        second_forward(half, 3)
    send(wo_all.at[c, z], wo_all.at[c, z], od_s.at[0], od_r.at[0], c=1 - c)
    for k, d in enumerate((1, -1)):
        send(wo_all.at[c, z], wo_all.at[c, z], oz_s.at[k], oz_r.at[k], z=around(z, d))
    for p in range(4):
        for half in range(2):
            a, b = where_a[half], where_b[half]
            for k in range(2):
                last = piece(half, around(a, offsets[p]), around(b, 2), k)
                arrived(last, *sems(half, 12 + p * 2 + k))
    for d in range(1, 4):
        arrived(nz.at[around(z, -d)], nyz_s.at[1, d], nyz_r.at[1, d])
    everything = ((nz[0] + nz[1]) + nz[2]) + nz[3]
    everything = jnp.sum(jnp.sum(everything, axis=1, keepdims=True), axis=0, keepdims=True)
    entries = HEADS * (NOPE + ROPE) + 2 * HEADS * NOPE + D
    norm_ref[...] = jnp.broadcast_to(jnp.sqrt(everything / entries), (8, 128))

    project(qs_ref, u_ref, cos_ref, sin_ref, abs_ref, qr_ref)

    def score(g, sc, scn):
        slot = lax.rem(g, SLOTS)
        scores_of(g, abs_ref, qr_ref, latn_ref, ropn_ref, lat_ref.at[slot], rop_ref.at[slot], sc, scn)

    def finish(g, sc, scn):
        attend(g, len_ref, latn_ref, lat_ref.at[lax.rem(g, SLOTS)], sc, scn, lo_ref)

    wait(0)
    score(0, sc0, scn0)

    def two(i, carry):
        g = i * 2

        @pl.when(g + 3 < GROUPS)
        def _():
            start(g + 3)

        wait(g + 1)
        score(g + 1, sc1, scn1)
        finish(g, sc0, scn0)

        @pl.when(g + 4 < GROUPS)
        def _():
            start(g + 4)

        @pl.when(g + 2 < GROUPS)
        def _():
            wait(g + 2)

        score(jnp.minimum(g + 2, GROUPS - 1), sc0, scn0)
        finish(g + 1, sc1, scn1)
        return carry

    def out_first():
        for k, d in enumerate((1, -1)):
            near = wo_all.at[c, around(z, -d)]
            arrived(near, oz_s.at[k], oz_r.at[k])
            part = wo_all.at[c, around(z, -d), pl.ds(k * 224, 224)]
            send(part, part, oz_s.at[2 + k], oz_r.at[2 + k], z=around(z, d))
            send(near, near, od_s.at[1 + k], od_r.at[1 + k], c=1 - c)

    def out_second():
        far = wo_all.at[c, around(z, 2)]
        for k in range(2):
            arrived(far.at[pl.ds(k * 224, 224)], oz_s.at[2 + k], oz_r.at[2 + k])
        send(far, far, od_s.at[3], od_r.at[3], c=1 - c)

    def out_ready():
        for n, d in enumerate((0, -1, 1, 2)):
            arrived(wo_all.at[1 - c, around(z, d)], od_s.at[n], od_r.at[n])

    def heads_done(j):
        rows = slice(j * 128, j * 128 + 128)
        for h in range(HL):
            if h < 5:
                up = u_ref[:, :, 96:128, 1024 + h * 128 : 1152 + h * 128].reshape(KVRANK, 128)
            else:
                up = u_ref[:, :, (h - 5) * 32 : (h - 4) * 32, 1536:1664].reshape(KVRANK, 128)
            both = nn(lo_ref[h, rows, :], up).astype(BF)
            for half in range(2):
                ho_ref[j, half, :, h * 128 : h * 128 + 128] = both[half * 64 : half * 64 + 64]
        hb_ref[j, y, c] = ho_ref[j, c]
        send(ho_ref.at[j, 1 - c], hb_ref.at[j, y, c], d2_s.at[j], d2_r.at[j], c=1 - c)
        for k, d in enumerate((1, -1)):
            send(
                ho_ref.at[j, c], hb_ref.at[j, y, c], hy_s.at[j, k], hy_r.at[j, k], y=around(y, d)
            )

    def partner_half(j):
        ref = hb_ref.at[j, y, 1 - c]
        arrived(ref, d2_s.at[j], d2_r.at[j])
        for k, d in enumerate((1, -1)):
            send(ref, ref, hy_s.at[j, 2 + k], hy_r.at[j, 2 + k], y=around(y, d))

    def pass_on(j):
        for k, d in enumerate((1, -1)):
            arrived(hb_ref.at[j, around(y, -d), c], hy_s.at[j, k], hy_r.at[j, k])
            arrived(hb_ref.at[j, around(y, -d), 1 - c], hy_s.at[j, 2 + k], hy_r.at[j, 2 + k])
            ref = hb_ref.at[j, around(y, -d), k]
            send(ref, ref, hy_s.at[j, 4 + k], hy_r.at[j, 4 + k], y=around(y, d))

    def multiply(j):
        for k in range(2):
            arrived(hb_ref.at[j, around(y, 2), k], hy_s.at[j, 4 + k], hy_r.at[j, 4 + k])

        def block(n):
            zs = lax.rem(x + n, 4)
            tokens = jnp.concatenate(
                [hb_ref[j, :, k].reshape(4 * HALF, 1024) for k in range(2)], axis=1
            )
            columns = jnp.concatenate([wo_all[k, zs] for k in range(2)], axis=1)
            ct_ref[j, zs] = nt(columns, tokens).astype(BF)

        block(2)
        for k, d in enumerate((1, -1)):
            send(
                ct_ref.at[j, around(x, 2), pl.ds(k * 224, 224)], r1_ref.at[j, k],
                r1_s.at[j, k], r1_r.at[j, k], x=around(x, d),
            )

        def rest(n, carry):
            block(jnp.where(n == 0, 1, jnp.where(n == 1, 3, 0)))
            return carry

        lax.fori_loop(0, 3, rest, 0)

    def add_far(j):
        for k, d in enumerate((1, -1)):
            arrived(r1_ref.at[j, k], r1_s.at[j, k], r1_r.at[j, k])
            rows = slice(k * 224, k * 224 + 224)
            near = around(x, d)
            both = ct_ref[j, near, rows].astype(F32) + r1_ref[j, k].astype(F32)
            ct_ref[j, near, rows] = both.astype(BF)
            send(ct_ref.at[j, near], rx_ref.at[j, k], r2_s.at[j, k], r2_r.at[j, k], x=near)

    returns = []

    def add_near(j):
        for k in range(2):
            arrived(rx_ref.at[j, k], r2_s.at[j, k], r2_r.at[j, k])
        fs_ref[j % 2] = (
            ct_ref[j, x].astype(F32) + rx_ref[j, 0].astype(F32) + rx_ref[j, 1].astype(F32)
        )
        if j % 2 == 0:
            return
        pair = j // 2
        lane = lax.broadcasted_iota(jnp.int32, (448, 128), 1)
        for v in range(2):
            early = fs_ref[0, :, v * 128 : v * 128 + 128]
            late = fs_ref[1, :, v * 128 : v * 128 + 128]
            ft_ref[pair, 2 * v] = jnp.where(lane < 64, early, pltpu.roll(late, 64, 1)).astype(BF)
            ft_ref[pair, 2 * v + 1] = jnp.where(lane < 64, pltpu.roll(early, 64, 1), late).astype(BF)
        target = ot_ref.at[
            pl.ds(pl.multiple_of(lax.rem(y, 2) * 448, 448), 448),
            pl.ds(pl.multiple_of((pair * 2 + c) * 128, 128), 128),
        ]
        own_core = y // 2
        for d in range(1, 4):
            to = around(y, d)
            send(
                ft_ref.at[pair, to], target, f_s.at[pair, d], f_r.at[pair, lax.rem(y, 2), c],
                y=to, c=own_core,
            )
        here = own_core == c

        @pl.when(here)
        def _():
            target[...] = ft_ref[pair, y]

        across = copy_to(
            ft_ref.at[pair, y], target, f_s.at[pair, 0], f_r.at[pair, lax.rem(y, 2), c], c=1 - c
        )

        @pl.when(jnp.logical_not(here))
        def _():
            across.start()

        returns.append((here, across))

    plan = {
        1: [(heads_done, 0)],
        2: [(partner_half, 0)],
        3: [(heads_done, 1), (pass_on, 0), (out_first,)],
        4: [(partner_half, 1)],
        5: [(heads_done, 2), (pass_on, 1), (out_second,)],
        6: [(partner_half, 2)],
        7: [(heads_done, 3), (pass_on, 2), (out_ready,), (multiply, 0)],
        8: [(partner_half, 3), (add_far, 0), (multiply, 1)],
        9: [(pass_on, 3), (add_near, 0), (add_far, 1), (multiply, 2)],
        10: [(multiply, 3), (add_near, 1), (add_far, 2)],
        11: [(add_near, 2), (add_far, 3)],
        12: [(add_near, 3)],
    }
    for slot in range(13):
        if slot < 8:
            lax.fori_loop(slot * 2, slot * 2 + 2, two, 0)
        for event, *which in plan.get(slot, []):
            event(*which)

    for pair in range(2):
        for ys in range(2):
            for cs in range(2):
                mine = (c * 2 + ys == y) & (c == cs)

                @pl.when(jnp.logical_not(mine))
                def _():
                    block = ot_ref.at[
                        ys * 448 : ys * 448 + 448, (pair * 2 + cs) * 128 : (pair * 2 + cs) * 128 + 128
                    ]
                    arrived(block, f_s.at[pair, 0], f_r.at[pair, ys, cs])

    def last(i, carry):
        rows = pl.ds(pl.multiple_of(i * 128, 128), 128)
        out_ref[rows, :] = nt(sel_ref[rows, :], ot_ref[...]).astype(BF)
        return carry

    lax.fori_loop(0, 4, last, 0)
    for made in sends:
        made.wait_send()
    for here, across in returns:

        @pl.when(jnp.logical_not(here))
        def _():
            across.wait_send()


def layer(uq, wk, wv, wo, q, latk, ropk, selk, sel, cos, sin, lengths, cache_latent, cache_rope):
    vmem = pl.BlockSpec(memory_space=pltpu.VMEM)
    hbm = pl.BlockSpec(memory_space=pl.ANY)
    dma = pltpu.SemaphoreType.DMA
    scratch = [
        ((8, 16, 1792), F32), ((8, 16, 1792), BF), ((8, 16, 1792), BF),
        ((8, 56, 1024), BF), ((8, 56, 1024), BF),
        ((4, 4, 128, 1664), BF), ((2, 4, 448, 1024), BF),
        ((3, 8, 128), F32), ((8, 8, 128), F32), ((4, 8, 128), F32), ((4, 8, 128), F32),
        ((TOK, QRANK), BF), ((TOK, KVRANK), BF), ((TOK, 256), BF),
        ((HL, TOK, KVRANK), BF), ((HL, TOK, 256), BF), ((HL, TOK, KVRANK), BF),
        ((SLOTS, 4, CACHE, KVRANK), BF), ((SLOTS, 4, ROPE, CACHE), BF),
        ((128, CACHE), F32), ((128, 16), F32), ((128, CACHE), F32), ((128, 16), F32),
        ((4, 2, HALF, 1024), BF), ((4, 4, 2, HALF, 1024), BF),
        ((4, 4, 448, 256), BF), ((4, 2, 224, 256), BF), ((4, 2, 448, 256), BF),
        ((2, 448, 256), F32), ((2, 4, 448, 128), BF), ((896, TOK), BF),
    ]
    counts = [
        (SLOTS,), (SLOTS,), (8,), (8,), (8,), (8,), (8,), (8,), (2, 4), (2, 4), (40,), (40,),
        (4,), (4,), (4,), (4,), (4,), (4,), (4, 6), (4, 6), (4, 2), (4, 2), (4, 2), (4, 2),
        (2, 4), (2, 2, 2),
    ]
    return pl.pallas_call(
        layer_kernel,
        out_shape=(jax.ShapeDtypeStruct((TOK, 896), BF), jax.ShapeDtypeStruct((8, 128), F32)),
        in_specs=[vmem] * 11 + [pl.BlockSpec(memory_space=pltpu.SMEM), hbm, hbm],
        out_specs=(vmem, vmem),
        scratch_shapes=[pltpu.VMEM(s, d) for s, d in scratch] + [dma(n) for n in counts],
        compiler_params=pltpu.CompilerParams(
            vmem_limit_bytes=67043328, collective_id=0, has_side_effects=True
        ),
        name="layer",
    )(uq, wk, wv, wo, q, latk, ropk, selk, sel, cos, sin, lengths, cache_latent, cache_rope)


def tables(lengths):
    half = ROPE // 2
    frequency = 10000.0 ** (-jnp.arange(half, dtype=F32) / half)
    frequency = jnp.tile(frequency, 4)
    positions = (lengths[:, None] + jnp.arange(NEWTOK, dtype=jnp.int32)[None, :]).reshape(TOK, 1)
    angles = positions.astype(F32) * frequency[None, :]
    sign = jnp.where(jnp.arange(128) % 64 < 32, -1.0, 1.0).astype(F32)
    return jnp.cos(angles), jnp.sin(angles) * sign[None, :]


def shards(q_latent, new_latent, new_rope, cache_latent, cache_rope, lengths, assignment, w_uq, w_uk, w_uv, w_o):
    slot_of = assignment[0]
    at = jnp.arange(TOK, dtype=jnp.int32)
    selk = (
        (jnp.tile(slot_of, NEWTOK)[None, :] == at[:, None] // 4)
        & (at[None, :] // SEQS == at[:, None] % 4)
    ).astype(BF)
    held = (at // 256) * 256 + ((at // 64) % 2) * 128 + ((at // 128) % 2) * 64 + at % 64
    sel = (
        (jnp.repeat(slot_of, NEWTOK)[:, None] == held[None, :] // 4)
        & (at[:, None] % 4 == held[None, :] % 4)
    ).astype(BF)
    cos, sin = tables(lengths)
    out, norm = layer(
        w_uq, w_uk, w_uv, w_o.T,
        q_latent.transpose(1, 0, 2).reshape(TOK, QRANK),
        new_latent.transpose(1, 0, 2).reshape(TOK, KVRANK),
        new_rope.transpose(1, 2, 0), selk, sel, cos, sin, lengths, cache_latent, cache_rope,
    )
    return out.reshape(SEQS, NEWTOK, 896), norm[0, 0:1]


def solution(mesh):
    split = Mesh(mesh.devices.reshape(4, 4, 4, 2), ("dp_0", "dp_1", "tp_0", "tp_1"))
    dp, tp = ("dp_0", "dp_1"), ("tp_0", "tp_1")
    placed = (
        P(dp, None, None), P(dp, None, None), P(dp, None, None), P(dp, None, None), P(dp, None, None),
        P(dp), P(dp, None), P(dp + tp, None), P(dp + tp, None), P(dp + tp, None), P(None, dp + tp),
    )
    return jax.shard_map(
        shards, mesh=split, in_specs=placed, out_specs=(P(dp, None, tp), P()), check_vma=False
    )
```

time: 330 us -> 160 us (0.48)
  Pallas kernels: 0 us -> 146 us
  waiting for transfers between devices: 90.8 us -> 0 us
  matrix products: 82.8 us -> 0 us
  blocking collectives: 52.9 us -> 0 us
  local copies, waits for them, and re-layouts: 45.3 us -> 8.84 us
  between operations: 18.7 us -> 0.68 us
  other arithmetic: 21.8 us -> 4 us
  starting transfers between devices: 14.6 us -> 0 us
    pallas_call x0 -> x1, Pallas kernels: none -> 146 us  [layer(): pl.pallas_call(layer_kernel, out_shape=(jax.ShapeDtypeStruct((TOK, 896),...]
    dot_general x14 -> x0, matrix products: 82.8 us -> none  [the longest x1 20.5 us: shards(): jnp.einsum('sqht,stc->sqhc', weights[..., :CACHE], cache_latent, preferre...]
    reduce_scatter x1 -> x0, waiting for transfers between devices: 43.5 us -> none  [shards(): reduced = lax.psum_scatter(partial_out, TP, scatter_dimension=1, tiled=True)]
    all_gather x2 -> x0, waiting for transfers between devices: 35.9 us -> none  [the longest x1 35.9 us: gather_together(): lines, at, finished = (lax.all_gather(ravelled, axis), 0, [])]
    psum x4 -> x0, blocking collectives: 34.9 us -> none  [over_axes(): value = lax.psum(value, axis)]
    all_to_all x1 -> x0, blocking collectives: 18 us -> none  [shards(): lax.all_to_all(out_cast, TP, split_axis=0, concat_axis=1, tiled=True)]
    all_to_all x3 -> x0, starting transfers between devices: 13.9 us -> none  [the longest x1 5.79 us: shards(): lax.all_to_all(key_cast, TP, split_axis=1, concat_axis=0, tiled=True)]
    all_to_all x3 -> x0, waiting for transfers between devices: 11.3 us -> none  [the longest x1 7.08 us: shards(): lax.all_to_all(query_cast, TP, split_axis=1, concat_axis=0, tiled=True)]
  transfers between devices with their start and end apart: 6 -> 0, of which waited for: 5 -> 0; matrix products, arithmetic and copies ran while one was open for 39% -> 0% of each run, Pallas kernels for 0% -> 0%
where the time goes in v1:
time: 160 us
  Pallas kernels  146 us (91%)
  local copies, waits for them, and re-layouts  8.84 us (6%)
  other arithmetic  4 us (2%)
    pallas_call x1, Pallas kernels, layer(): pl.pallas_call(layer_kernel, out_shape=(jax.ShapeDtypeStruct((TOK, 896),...  146 us

profile of v1, /device:TPU:1, one launch (start us, length us, event | category | flops | bytes accessed | tf_op | source)
XLA Modules:
  0.0 159.7 jit_solution(14627946306636773255)
XLA Ops:
  0.6 0.0 copy-start
  0.7 0.1 mul.69
  0.8 0.8 broadcast_bitcast_fusion
  1.5 0.7 broadcast_in_dim.8
  2.3 0.1 eq.74
  2.4 0.7 add_convert_fusion
  3.1 0.1 convert_element_type.20
  3.2 1.9 %fusion = (f32[512,128]{1,0:T(8,128)}, f32[512,128]{1,0:T(8,128)}) fusion(f32[128]{0:T(128)S(1)} %compare_select_fusion, f32[128]{0:T(128)S(1)} %mul.69, f32[512]{0:T(512)S(1)} %convert_element_type.20), kind=kLoop, calls=%fused_computation.4 | loop fusion | flops 131072 | bytes 527360 | tf_op jit(solution)/shard_map/mul | solution.py:617
  5.1 1.9 %copy.16 = bf16[4,128,512]{2,1,0:T(8,128)(2,1)} copy(bf16[4,128,512]{2,0,1:T(4,128)(2,1)} %bitcast.14) | data formatting | bytes 1048576 | tf_op jit(solution)/shard_map/transpose | solution.py:636
  7.0 1.4 and_convert_fusion
  8.4 0.0 copy-done
  8.4 1.4 copy.15
  9.8 146.2 %layer.1 = (bf16[512,896]{1,0:T(8,128)(2,1)}, f32[8,128]{1,0:T(8,128)}) custom-call(f32[12,12288]{1,0:T(8,128)} %uq_ref.1, f32[4,8192]{1,0:T(4,128)} %wk_ref.1, f32[4,8192]{1,0:T(4,128)} %wv_ref.1, f32[56,8192]{1,0:T(8,128)} %bitcast.12, bf16[512,1536]{1,0:T(8,128)(2,1)} %bitcast.10, bf16[512,512]{1,0:T(8,128)(2,1)} %bitcast.11, ...), custom_call_target="tpu_custom_call" | custom-call | tf_op jit(solution)/shard_map/layer/pallas_call | solution.py:597
  156.0 1.2 slice.3
  157.2 2.5 %reshape.249 = bf16[128,4,896]{2,1,0:T(4,128)(2,1)} reshape(bf16[512,896]{1,0:T(8,128)(2,1)} %get-tuple-element.4) | data formatting | bytes 1835008 | tf_op jit(solution)/shard_map/reshape | solution.py:639
  (6 shorter events, 0.1 us)
Async XLA Ops:
  0.6 7.8 %copy-start = (bf16[128,4,1536]{2,1,0:T(4,128)(2,1)S(1)}, bf16[128,4,1536]{2,1,0:T(4,128)(2,1)}, u32[]{:S(2)}) copy-start(bf16[128,4,1536]{2,1,0:T(4,128)(2,1)} %param.11) | copy-start | bytes 4718596

commit v2 on v1

v2 whole, which is shorter than its diff:
```python
import jax
import jax.numpy as jnp
import numpy as np
from jax import lax
from jax.experimental import pallas as pl
from jax.experimental.pallas import tpu as pltpu
from jax.sharding import Mesh
from jax.sharding import PartitionSpec as P

D = 7168
QRANK = 1536
KVRANK = 512
NOPE = 128
ROPE = 64
VDIM = 128
HEADS = 64
NEWTOK = 4
CACHE = 256
SEQS = 128
TOK = SEQS * NEWTOK
HL = 8
GROUPS = SEQS // 4
SLOTS = 4
BF = jnp.bfloat16
F32 = jnp.float32
DP_TP = ("dp_0", "dp_1", "tp_0", "tp_1")
TP = ("tp_0", "tp_1")
DP = ("dp_0", "dp_1")
SCALE = (NOPE + ROPE) ** (-0.5)


def nt(a, b):
    return lax.dot_general(a, b, (((1,), (1,)), ((), ())), preferred_element_type=F32)


def nn(a, b):
    return lax.dot_general(a, b, (((1,), (0,)), ((), ())), preferred_element_type=F32)


def project(q_ref, u_ref, cos_ref, sin_ref, abs_ref, qr_ref, part):
    def nope_pair(i):
        cols = pl.ds(i * 256, 256)
        both = nn(q_ref[...], u_ref[:, 0:96, cols].reshape(QRANK, 256)).astype(BF)
        for j in range(2):
            own_cols = pl.ds(i * 256 + j * 128, 128)
            keys = u_ref[:, 96:128, own_cols].reshape(KVRANK, 128)
            abs_ref[i * 2 + j] = nt(both[:, j * 128 : (j + 1) * 128], keys).astype(BF)

    lane = lax.broadcasted_iota(jnp.int32, (TOK, 128), 1)
    row = lax.broadcasted_iota(jnp.int32, (TOK, 128), 0)
    own = lax.rem(row // 4, 4)
    low = lax.rem(lane, 64) < 32

    def quad(i):
        nope_pair(2 * i)
        nope_pair(2 * i + 1)
        if i == 0:
            pe_cols = u_ref[:, 0:96, 1024:1280].reshape(QRANK, 256)
        else:
            tail = [u_ref[:, 96:128, 1024 + b * 128 : 1152 + b * 128] for b in range(3)]
            pe_cols = jnp.concatenate(
                [
                    u_ref[:, 0:96, 1280:1408].reshape(QRANK, 128),
                    jnp.concatenate(tail, axis=1).reshape(QRANK, 128),
                ],
                axis=1,
            )
        four = nn(q_ref[...], pe_cols).astype(BF).astype(F32)
        for j in range(2):
            pe = four[:, j * 128 : (j + 1) * 128]
            other = jnp.where(low, pltpu.roll(pe, 96, 1), pltpu.roll(pe, 32, 1))
            rot = pe * cos_ref[...] + other * sin_ref[...]
            flip = pltpu.roll(rot, 64, 1)
            for odd in range(2):
                twice = jnp.where((lane < 64) == (odd == 0), rot, flip)
                head = i * 4 + j * 2 + odd
                for half in range(2):
                    kept = jnp.where(own == 2 * half + lane // 64, twice, 0.0)
                    qr_ref[head, :, half * 128 : (half + 1) * 128] = kept.astype(BF)

    quad(part)


def scores_of(g, abs_ref, qr_ref, latn_ref, ropn_ref, lat, rop, sc_ref, scn_ref):
    rows = pl.ds(pl.multiple_of(g * 16, 16), 16)
    q = abs_ref[:, rows, :].reshape(128, KVRANK)
    qr = qr_ref[:, rows, :].reshape(128, 256)
    seq = lax.rem(lax.broadcasted_iota(jnp.int32, (128, KVRANK), 0) // 4, 4)
    zero = jnp.zeros_like(q)
    parts = jnp.concatenate([jnp.where(seq == s, q, zero) for s in range(4)], axis=1)
    keys = jnp.concatenate([lat[s] for s in range(4)], axis=1)
    sc_ref[...] = nt(parts, keys) + nn(qr, rop[...].reshape(256, CACHE))
    scn_ref[...] = nt(q, latn_ref[rows, :]) + nt(qr, ropn_ref[rows, :])


def attend(g, len_ref, latn_ref, lat, sc_ref, scn_ref, lo_ref):
    row = lax.broadcasted_iota(jnp.int32, (128, CACHE), 0)
    seq = lax.rem(row // 4, 4)
    limit = jnp.where(
        seq == 0,
        len_ref[g * 4],
        jnp.where(
            seq == 1, len_ref[g * 4 + 1], jnp.where(seq == 2, len_ref[g * 4 + 2], len_ref[g * 4 + 3])
        ),
    )
    at = lax.broadcasted_iota(jnp.int32, (128, CACHE), 1)
    sc = jnp.where(at < limit, sc_ref[...] * SCALE, -jnp.inf)
    nrow = lax.broadcasted_iota(jnp.int32, (128, 16), 0)
    ncol = lax.broadcasted_iota(jnp.int32, (128, 16), 1)
    fits = (lax.rem(nrow // 4, 4) == ncol // 4) & (lax.rem(ncol, 4) <= lax.rem(nrow, 4))
    scn = jnp.where(fits, scn_ref[...] * SCALE, -jnp.inf)
    top = jnp.maximum(
        jnp.max(sc, axis=1, keepdims=True), jnp.max(scn, axis=1, keepdims=True)
    )
    ex = jnp.exp(sc - top)
    exn = jnp.exp(scn - top)
    total = jnp.sum(ex, axis=1, keepdims=True) + jnp.sum(exn, axis=1, keepdims=True)
    share = 1.0 / total
    w = (ex * share).astype(BF)
    wn = (exn * share).astype(BF)
    zero = jnp.zeros_like(w)
    parts = jnp.concatenate([jnp.where(seq == s, w, zero) for s in range(4)], axis=1)
    rows = pl.ds(pl.multiple_of(g * 16, 16), 16)
    out = nn(parts, lat[...].reshape(4 * CACHE, KVRANK)) + nn(wn, latn_ref[rows, :])
    lo_ref[:, rows, :] = out.astype(BF).reshape(HL, 16, KVRANK)


MESH = pl.DeviceIdType.MESH
CHUNKS = 4
HALF = 64


def around(i, d):
    return lax.rem(i + d + 4, 4)


def layer_kernel(
    ropk_ref, asn_ref, lenv_ref, freq_ref, len_ref,
    uq_hbm, wk_hbm, wv_hbm, wo_hbm, q_hbm, latk_hbm, lat_hbm, rop_hbm,
    out_hbm, sel_hbm, norm_ref,
    uq_ref, wk_ref, wv_ref, wo_ref, q_ref, latk_ref, selk_ref, sel_ref, cos_ref, sin_ref,
    stage, packs, rp, opack, orp, u_ref, v_ref, wo_all, nsend, ntp, ny, nz,
    qs_ref, latn_ref, ropn_ref, abs_ref, qr_ref, lo_ref, lat_ref, rop_ref, sc0, scn0, sc1, scn1,
    ho_ref, hb_ref, ct_ref, r1_ref, rx_ref, fs_ref, ft_ref, ot_ref,
    in_sem, lat_sem, rop_sem, a2a_sem, o2a_sem, nt_sem, nyz_sem, ag_s, ag_r, uv_s, uv_r,
    oz_sem, od_sem, d2_s, d2_r, hy_s, hy_r, r1_s, r1_r, r2_s, r2_r, f_sem,
):
    z, y = lax.axis_index("dp_0"), lax.axis_index("dp_1")
    x, c = lax.axis_index("tp_0"), lax.axis_index("tp_1")
    t = x * 2 + c
    def copy_to(src, dst, ss, rs, **axes):
        names = {"z": "dp_0", "y": "dp_1", "x": "tp_0", "c": "tp_1"}
        return pltpu.make_async_remote_copy(
            src_ref=src, dst_ref=dst, send_sem=ss, recv_sem=rs,
            device_id={names[n]: v for n, v in axes.items()}, device_id_type=MESH,
        )

    def send(src, dst, ss, rs, **axes):
        copy_to(src, dst, ss, rs, **axes).start()

    def arrived(dst, rs):
        copy_to(dst, dst, rs, rs, c=1 - c).wait_recv()

    def left(src, ss):
        copy_to(src, src, ss, ss, c=1 - c).wait_send()

    barrier = pltpu.get_barrier_semaphore()

    def greet(**axes):
        names = {"z": "dp_0", "y": "dp_1", "x": "tp_0", "c": "tp_1"}
        pl.semaphore_signal(
            barrier, inc=1, device_id={names[n]: v for n, v in axes.items()}, device_id_type=MESH
        )

    for dt in range(1, 8):
        peer = lax.rem(t + dt, 8)
        greet(x=peer // 2, c=lax.rem(peer, 2))
    for d in range(1, 4):
        greet(z=around(z, d))
        greet(y=around(y, d))
        greet(y=around(y, d), c=1 - c)

    loads = []
    for n, (src, dst) in enumerate(
        (
            (uq_hbm, uq_ref), (wk_hbm, wk_ref), (wv_hbm, wv_ref), (wo_hbm, wo_ref), (q_hbm, q_ref),
            (latk_hbm, latk_ref),
        )
    ):
        loads.append(pltpu.make_async_copy(src, dst, in_sem.at[n]))
        loads[n].start()

    def fetch(g):
        slot = lax.rem(g, SLOTS)
        return (
            pltpu.make_async_copy(lat_hbm.at[pl.ds(g * 4, 4)], lat_ref.at[slot], lat_sem.at[slot]),
            pltpu.make_async_copy(rop_hbm.at[pl.ds(g * 4, 4)], rop_ref.at[slot], rop_sem.at[slot]),
        )

    def start(g):
        for made in fetch(g):
            made.start()

    def wait(g):
        for made in fetch(g):
            made.wait()

    for g in range(SLOTS - 1):
        start(g)

    lane12 = lax.broadcasted_iota(jnp.int32, (12, 128), 1)

    def fold(v):
        rows, cols = v.shape
        total = jnp.zeros((8, 128), F32)
        for i in range(rows // 8):
            for j in range(cols // 128):
                part = v[i * 8 : i * 8 + 8, j * 128 : j * 128 + 128]
                total = total + part * part
        return total

    def pack_one(p, squares):
        for i in range(4):
            v = uq_ref[:, pl.ds(pl.multiple_of(p * 1536 + i * 384, 128), 384)]
            v0, v1, v2 = v[:, 0:128], v[:, 128:256], v[:, 256:384]
            stage[p, 0:12, i * 256 : i * 256 + 128] = v0
            stage[p, 0:12, i * 256 + 128 : i * 256 + 256] = pltpu.roll(
                jnp.where(lane12 < 64, v2, v1), 64, 1
            )
            stage[p, 0:12, 1024 + i * 128 : 1152 + i * 128] = jnp.where(lane12 < 64, v1, v2)
            stage[p, i * 4 : i * 4 + 4, 1536:1792] = wv_ref[
                :, pl.ds(pl.multiple_of(p * 1024 + i * 256, 128), 256)
            ]
        stage[p, 12:16, 0:1024] = wk_ref[:, pl.ds(pl.multiple_of(p * 1024, 128), 1024)]
        stage[p, 12:16, 1024:1536] = jnp.zeros((4, 512), F32)
        whole = stage[p]
        packs[p] = whole.astype(BF)
        return squares + fold(whole)

    for n in range(3):
        loads[n].wait()
    squares = lax.fori_loop(0, 8, pack_one, jnp.zeros((8, 128), F32))
    pl.semaphore_wait(barrier, 16)
    for dt in range(1, 8):
        peer = lax.rem(t + dt, 8)
        send(
            packs.at[peer], rp.at[t], a2a_sem.at[0], a2a_sem.at[1], x=peer // 2, c=lax.rem(peer, 2)
        )
    rp[t] = packs[t]

    def pack_out(p, squares):
        v = wo_ref[:, pl.ds(pl.multiple_of(p * 1024, 128), 1024)]
        opack[p] = v.astype(BF)
        return squares + fold(v)

    loads[3].wait()
    squares = lax.fori_loop(0, 8, pack_out, squares)
    nsend[0] = squares
    ntp[t] = squares
    for dt in range(1, 8):
        peer = lax.rem(t + dt, 8)
        where = dict(x=peer // 2, c=lax.rem(peer, 2))
        send(nsend.at[0], ntp.at[t], nt_sem.at[0], nt_sem.at[1], **where)
        send(opack.at[peer], orp.at[t], o2a_sem.at[0], o2a_sem.at[1], **where)
    orp[t] = opack[t]

    row = lax.broadcasted_iota(jnp.int32, (TOK, TOK), 0)
    col = lax.broadcasted_iota(jnp.int32, (TOK, TOK), 1)
    spread = jnp.where(
        lax.broadcasted_iota(jnp.int32, (SEQS, TOK), 0)
        == lax.broadcasted_iota(jnp.int32, (SEQS, TOK), 1) // NEWTOK, 1.0, 0.0,
    ).astype(BF)
    slot_of = jnp.broadcast_to(asn_ref[...], (8, SEQS)).astype(F32)
    slot_by_token = nn(slot_of.astype(BF), spread)[0:1, :].astype(jnp.int32)
    slot_tiled = jnp.concatenate([asn_ref[...]] * NEWTOK, axis=1)
    selk_ref[0] = jnp.where(
        (slot_tiled == row // 4) & (col // SEQS == lax.rem(row, 4)), 1.0, 0.0
    ).astype(BF)
    same_token = lax.rem(row, 4) == lax.rem(col, 4)
    selk_ref[1] = jnp.where((slot_by_token == row // 4) & same_token, 1.0, 0.0).astype(BF)
    held = (
        (row // 256) * 256 + lax.rem(row // 64, 2) * 128 + lax.rem(row // 128, 2) * 64
        + lax.rem(row, 64)
    )
    back = jnp.where((slot_by_token == held // 4) & same_token, 1.0, 0.0).astype(BF)
    identity = jnp.where(row == col, 1.0, 0.0).astype(BF)
    sel_ref[...] = nt(identity, back).astype(BF)
    keep_sel = pltpu.make_async_copy(sel_ref, sel_hbm, in_sem.at[6])
    keep_out = pltpu.make_async_copy(ot_ref, out_hbm, in_sem.at[7])
    lengths_wide = jnp.broadcast_to(lenv_ref[...], (SEQS, SEQS)).astype(F32).astype(BF)

    def rotation(i, carry):
        rows = pl.ds(pl.multiple_of(i * 128, 128), 128)
        r = lax.broadcasted_iota(jnp.int32, (128, 128), 0) + i * 128
        lane = lax.broadcasted_iota(jnp.int32, (128, 128), 1)
        pick = jnp.where(r // 4 == lane, 1.0, 0.0).astype(BF)
        positions = nt(pick, lengths_wide) + lax.rem(r, 4).astype(F32)
        angles = positions * freq_ref[0:1, :]
        cos_ref[rows, :] = jnp.cos(angles)
        sine = jnp.sin(angles)
        sin_ref[rows, :] = jnp.where(lax.rem(lane, 64) < 32, -sine, sine)
        return carry

    arrived(rp.at[0:7], a2a_sem.at[1])
    big = rp[...].reshape(128, 1792)
    r = lax.broadcasted_iota(jnp.int32, (128, 128), 0)
    col = lax.broadcasted_iota(jnp.int32, (128, 128), 1)
    origin = jnp.where(
        r < 96, (r // 12) * 16 + lax.rem(r, 12), ((r - 96) // 4) * 16 + 12 + lax.rem(r - 96, 4)
    )
    order = jnp.where(col == origin, 1.0, 0.0).astype(BF)
    sorted_rows = nn(order, big[:, 0:1536]).astype(BF)
    r32 = lax.broadcasted_iota(jnp.int32, (32, 128), 0)
    col32 = lax.broadcasted_iota(jnp.int32, (32, 128), 1)
    uv_parts = []
    for i in range(4):
        pick = jnp.where(col32 == (r32 // 4) * 16 + i * 4 + lax.rem(r32, 4), 1.0, 0.0).astype(BF)
        uv_parts.append(nn(pick, big[:, 1536:1792]).astype(BF))
    me = z * 4 + y
    u_ref[me, 0:96] = sorted_rows[0:96, 0:1408]
    u_ref[me, 96:128, 0:1024] = sorted_rows[96:128, 0:1024]
    for i in range(3):
        u_ref[me, 96:128, 1024 + i * 128 : 1152 + i * 128] = sorted_rows[
            i * 32 : i * 32 + 32, 1408:1536
        ]
    v_ref[me] = jnp.concatenate(uv_parts, axis=1)

    def piece(ring, ia, ib, sub=None):
        if ring == 2:
            at = v_ref.at[ia * 4 + ib]
            return at if sub is None else at.at[:, pl.ds(sub * 512, 512)]
        rows = pl.ds(ring * 64, 64) if sub is None else pl.ds(ring * 64 + sub * 32, 32)
        return u_ref.at[ib * 4 + ia if ring == 0 else ia * 4 + ib, rows]

    def step(ring, along_first, to):
        first, second = ("y", "z") if ring == 0 else ("z", "y")
        return {first if along_first else second: to}

    where_a = [y, z, z]
    where_b = [z, y, y]

    def sent(ring):
        return ag_s.at[0] if ring < 2 else uv_s.at[0]

    def got(ring, n):
        if ring == 2:
            return uv_r.at[min(n, 12)]
        return ag_r.at[24 if n >= 12 else ring * 12 + n]

    offsets = (0, -1, 1, 2)

    def first_send(ring):
        a, b = where_a[ring], where_b[ring]
        for k, d in enumerate((1, -1)):
            ref = piece(ring, a, b)
            send(ref, ref, sent(ring), got(ring, k), **step(ring, True, around(a, d)))

    def first_forward(ring):
        a, b = where_a[ring], where_b[ring]
        for k, d in enumerate((1, -1)):
            arrived(piece(ring, around(a, -d), b), got(ring, k))
            ref = piece(ring, around(a, -d), b, k)
            send(ref, ref, sent(ring), got(ring, 2 + k), **step(ring, True, around(a, d)))

    def first_last(ring):
        a, b = where_a[ring], where_b[ring]
        for k in range(2):
            arrived(piece(ring, around(a, 2), b, k), got(ring, 2 + k))

    def second_send(ring, p):
        a, b = where_a[ring], where_b[ring]
        ia = around(a, offsets[p])
        for k, d in enumerate((1, -1)):
            ref = piece(ring, ia, b)
            send(ref, ref, sent(ring), got(ring, 4 + p * 2 + k), **step(ring, False, around(b, d)))

    def second_forward(ring, p):
        a, b = where_a[ring], where_b[ring]
        ia = around(a, offsets[p])
        for k, d in enumerate((1, -1)):
            arrived(piece(ring, ia, around(b, -d)), got(ring, 4 + p * 2 + k))
            ref = piece(ring, ia, around(b, -d), k)
            send(ref, ref, sent(ring), got(ring, 12), **step(ring, False, around(b, d)))

    for ring in range(2):
        first_send(ring)
    for ring in range(2):
        second_send(ring, 0)

    loads[4].wait()
    loads[5].wait()
    keep_sel.start()

    def move_q(i, carry):
        cols = pl.ds(pl.multiple_of(i * 256, 256), 256)
        qs_ref[:, cols] = nn(selk_ref[1], q_ref[:, :, cols].reshape(TOK, 256)).astype(BF)
        return carry

    lax.fori_loop(0, QRANK // 256, move_q, 0)
    lax.fori_loop(0, 4, rotation, 0)

    arrived(ntp.at[0:7], nt_sem.at[1])
    line = ntp[0]
    for i in range(1, 8):
        line = line + ntp[i]
    latn_ref[...] = nn(selk_ref[1], latk_ref[...].reshape(TOK, KVRANK)).astype(BF)
    rope_rows = jnp.concatenate([ropk_ref[k] for k in range(4)], axis=1)
    ropn_ref[...] = nt(selk_ref[0], jnp.concatenate([rope_rows] * 4, axis=0)).astype(BF)
    nsend[1] = line
    ny[y] = line
    for d in range(1, 4):
        send(nsend.at[1], ny.at[y], nyz_sem.at[0], nyz_sem.at[1], y=around(y, d))

    for ring in range(2):
        first_forward(ring)
    for ring in range(2):
        second_send(ring, 1)
        second_send(ring, 2)
    first_send(2)
    for ring in range(2):
        second_forward(ring, 0)
    arrived(ny.at[0:3], nyz_sem.at[1])
    plane = ((ny[0] + ny[1]) + ny[2]) + ny[3]
    nsend[2] = plane
    nz[z] = plane
    for d in range(1, 4):
        send(nsend.at[2], nz.at[z], nyz_sem.at[0], nyz_sem.at[2], z=around(z, d))
    for ring in range(2):
        first_last(ring)
        second_send(ring, 3)
    first_forward(2)
    for p in range(1, 3):
        for ring in range(2):
            second_forward(ring, p)

    arrived(orp.at[0:7], o2a_sem.at[1])
    wo_all[c, z] = jnp.concatenate([orp[i].astype(F32) for i in range(8)], axis=0).astype(BF)
    first_last(2)
    for ring in range(2):
        second_forward(ring, 3)
    for p in range(4):
        second_send(2, p)
    send(wo_all.at[c, z], wo_all.at[c, z], od_sem.at[0], od_sem.at[1], c=1 - c)
    for later in range(2):
        for k, d in enumerate((1, -1)):
            part = wo_all.at[c, z, pl.ds((k ^ later) * 224, 224)]
            send(part, part, oz_sem.at[0], oz_sem.at[1 + later], z=around(z, d))
    arrived(u_ref.at[0:4], ag_r.at[24])
    arrived(nz.at[0:3], nyz_sem.at[2])
    everything = ((nz[0] + nz[1]) + nz[2]) + nz[3]
    everything = jnp.sum(jnp.sum(everything, axis=1, keepdims=True), axis=0, keepdims=True)
    entries = HEADS * (NOPE + ROPE) + 2 * HEADS * NOPE + D
    norm_ref[0] = jnp.sqrt(everything / entries)[0, 0]

    project(qs_ref, u_ref, cos_ref, sin_ref, abs_ref, qr_ref, 0)
    second_forward(2, 0)
    second_forward(2, 1)
    project(qs_ref, u_ref, cos_ref, sin_ref, abs_ref, qr_ref, 1)
    second_forward(2, 2)

    def score(g, sc, scn):
        slot = lax.rem(g, SLOTS)
        scores_of(g, abs_ref, qr_ref, latn_ref, ropn_ref, lat_ref.at[slot], rop_ref.at[slot], sc, scn)

    def finish(g, sc, scn):
        attend(g, len_ref, latn_ref, lat_ref.at[lax.rem(g, SLOTS)], sc, scn, lo_ref)

    wait(0)
    score(0, sc0, scn0)

    def two(i):
        g = i * 2

        @pl.when(g + 3 < GROUPS)
        def _():
            start(g + 3)

        wait(g + 1)
        score(g + 1, sc1, scn1)
        finish(g, sc0, scn0)

        @pl.when(g + 4 < GROUPS)
        def _():
            start(g + 4)

        @pl.when(g + 2 < GROUPS)
        def _():
            wait(g + 2)

        score(jnp.minimum(g + 2, GROUPS - 1), sc0, scn0)
        finish(g + 1, sc1, scn1)

    def values_pass():
        second_forward(2, 3)

    def values_ready():
        arrived(v_ref.at[0:4], uv_r.at[12])

    def out_pass():
        arrived(wo_all.at[c, z], oz_sem.at[1])
        for k, d in enumerate((1, -1)):
            part = wo_all.at[c, around(z, -d), pl.ds(k * 224, 224)]
            send(part, part, oz_sem.at[0], oz_sem.at[3], z=around(z, d))

    def out_near():
        arrived(wo_all.at[c, z], oz_sem.at[2])
        for d in (1, -1):
            near = wo_all.at[c, around(z, d)]
            send(near, near, od_sem.at[0], od_sem.at[1], c=1 - c)

    def out_far():
        far = wo_all.at[c, around(z, 2)]
        arrived(far, oz_sem.at[3])
        send(far, far, od_sem.at[0], od_sem.at[1], c=1 - c)

    def out_ready():
        arrived(wo_all.at[1 - c], od_sem.at[1])

    def head_values(j):
        rows = slice(j * 128, j * 128 + 128)
        for h in range(HL):
            up = v_ref[:, :, h * 128 : h * 128 + 128].reshape(KVRANK, 128)
            both = nn(lo_ref[h, rows, :], up).astype(BF)
            for half in range(2):
                ho_ref[j, half, :, h * 128 : h * 128 + 128] = both[half * 64 : half * 64 + 64]
        hb_ref[j, y, c] = ho_ref[j, c]

    def heads_done(j):
        head_values(j)
        send(ho_ref.at[j, 1 - c], hb_ref.at[j, y, c], d2_s.at[0], d2_r.at[j], c=1 - c)
        for d in (1, -1):
            send(ho_ref.at[j, c], hb_ref.at[j, y, c], hy_s.at[0], hy_r.at[j, 0], y=around(y, d))

    def partner_half(j):
        ref = hb_ref.at[j, y, 1 - c]
        arrived(ref, d2_r.at[j])
        for d in (1, -1):
            send(ref, ref, hy_s.at[0], hy_r.at[j, 0], y=around(y, d))

    def pass_on(j):
        arrived(hb_ref.at[j, 0:2], hy_r.at[j, 0])
        for k, d in enumerate((1, -1)):
            ref = hb_ref.at[j, around(y, -d), k]
            send(ref, ref, hy_s.at[0], hy_r.at[j, 1], y=around(y, d))

    def multiply(j):
        arrived(hb_ref.at[j, around(y, 2)], hy_r.at[j, 1])

        def block(n):
            zs = lax.rem(x + n, 4)
            tokens = jnp.concatenate(
                [hb_ref[j, :, k].reshape(4 * HALF, 1024) for k in range(2)], axis=1
            )
            columns = jnp.concatenate([wo_all[k, zs] for k in range(2)], axis=1)
            ct_ref[j, zs] = nt(columns, tokens).astype(BF)

        block(2)
        for k, d in enumerate((1, -1)):
            send(
                ct_ref.at[j, around(x, 2), pl.ds(k * 224, 224)], r1_ref.at[j, k],
                r1_s.at[0], r1_r.at[j], x=around(x, d),
            )

        def rest(n, carry):
            block(jnp.where(n == 0, 1, jnp.where(n == 1, 3, 0)))
            return carry

        lax.fori_loop(0, 3, rest, 0)

    def add_far(j):
        arrived(r1_ref.at[j], r1_r.at[j])
        for k, d in enumerate((1, -1)):
            rows = slice(k * 224, k * 224 + 224)
            near = around(x, d)
            both = ct_ref[j, near, rows].astype(F32) + r1_ref[j, k].astype(F32)
            ct_ref[j, near, rows] = both.astype(BF)
            send(ct_ref.at[j, near], rx_ref.at[j, k], r2_s.at[0], r2_r.at[j], x=near)

    def collect(j):
        fs_ref[j % 2] = (
            ct_ref[j, x].astype(F32) + rx_ref[j, 0].astype(F32) + rx_ref[j, 1].astype(F32)
        )
        if j % 2 == 0:
            return
        lane = lax.broadcasted_iota(jnp.int32, (448, 128), 1)
        for v in range(2):
            early = fs_ref[0, :, v * 128 : v * 128 + 128]
            late = fs_ref[1, :, v * 128 : v * 128 + 128]
            ft_ref[j // 2 * 4 + 2 * v] = jnp.where(lane < 64, early, pltpu.roll(late, 64, 1)).astype(BF)
            ft_ref[j // 2 * 4 + 2 * v + 1] = jnp.where(lane < 64, pltpu.roll(early, 64, 1), late).astype(BF)

    here = y // 2 == c

    def add_near(j):
        arrived(rx_ref.at[j], r2_r.at[j])
        collect(j)
        if j % 2 == 0:
            return
        pair = j // 2
        target = ot_ref.at[
            pl.ds(pl.multiple_of(lax.rem(y, 2) * 448, 448), 448),
            pl.ds(pl.multiple_of((pair * 2 + c) * 128, 128), 128),
        ]
        for d in (2, 1, 3):
            to = around(y, d)
            send(ft_ref.at[pair * 4 + to], target, f_sem.at[0], f_sem.at[1], y=to, c=y // 2)

        @pl.when(here)
        def _():
            target[...] = ft_ref[pair * 4 + y]

        @pl.when(jnp.logical_not(here))
        def _():
            send(ft_ref.at[pair * 4 + y], target, f_sem.at[2], f_sem.at[1], c=1 - c)

    plan = {
        0: [(values_pass,), (out_pass,)],
        3: [(values_ready,), (heads_done, 0)],
        4: [(partner_half, 0)],
        6: [(out_near,)],
        7: [(pass_on, 0), (heads_done, 1)],
        8: [(partner_half, 1)],
        11: [(heads_done, 2), (out_far,)],
        12: [(pass_on, 1), (partner_half, 2), (out_ready,), (multiply, 0)],
        13: [(add_far, 0)],
        14: [(multiply, 1)],
        15: [(pass_on, 2), (heads_done, 3)],
        16: [(add_near, 0), (partner_half, 3), (add_far, 1)],
        17: [(multiply, 2)],
        18: [(pass_on, 3), (add_near, 1), (add_far, 2)],
        19: [(multiply, 3)],
        20: [(add_near, 2), (add_far, 3), (add_near, 3)],
    }

    def run(events):
        for event, *which in events:
            event(*which)

    def together(i, carry):
        two(i)
        for slot in range(16):
            if slot in plan:

                @pl.when(i == slot)
                def _():
                    run(plan[slot])

        return carry

    lax.fori_loop(0, 16, together, 0)
    for slot in range(16, 21):
        run(plan[slot])

    @pl.when(here)
    def _():
        arrived(ft_ref.at[0:6], f_sem.at[1])

    @pl.when(jnp.logical_not(here))
    def _():
        arrived(ft_ref.at[0:8], f_sem.at[1])

    keep_out.start()
    left(packs.at[0:7], a2a_sem.at[0])
    left(opack.at[0:7], o2a_sem.at[0])
    left(ntp.at[0:7], nt_sem.at[0])
    left(ntp.at[0:6], nyz_sem.at[0])
    left(u_ref.at[0:15], ag_s.at[0])
    left(v_ref.at[0:15], uv_s.at[0])
    left(wo_all.at[0, 0:3], oz_sem.at[0])
    left(wo_all.at[0], od_sem.at[0])
    left(ho_ref.at[0:2], d2_s.at[0])
    left(hb_ref.at[0:3], hy_s.at[0])
    left(ct_ref.at[0], r1_s.at[0])
    left(ct_ref.at[0:2], r2_s.at[0])
    left(ft_ref.at[0:6], f_sem.at[0])

    @pl.when(jnp.logical_not(here))
    def _():
        left(ft_ref.at[0:2], f_sem.at[2])

    keep_sel.wait()
    keep_out.wait()


def place_kernel(sel_ref, held_ref, out_ref):
    placed = nt(sel_ref[...], held_ref[...]).astype(BF)
    out_ref[...] = placed.reshape(32, 4, 896)


def layer(uq, wk, wv, wo, q, latk, ropk, slot_of, lengths, frequency, cache_latent, cache_rope):
    vmem = pl.BlockSpec(memory_space=pltpu.VMEM)
    smem = pl.BlockSpec(memory_space=pltpu.SMEM)
    hbm = pl.BlockSpec(memory_space=pl.ANY)
    dma = pltpu.SemaphoreType.DMA
    scratch = [
        ((12, 12288), F32), ((4, 8192), F32), ((4, 8192), F32), ((56, 8192), F32),
        ((SEQS, 4, QRANK), BF), ((SEQS, 4, KVRANK), BF), ((2, TOK, TOK), BF), ((TOK, TOK), BF),
        ((TOK, 128), F32), ((TOK, 128), F32),
        ((8, 16, 1792), F32), ((8, 16, 1792), BF), ((8, 16, 1792), BF),
        ((8, 56, 1024), BF), ((8, 56, 1024), BF),
        ((16, 128, 1408), BF), ((16, 32, 1024), BF), ((2, 4, 448, 1024), BF),
        ((3, 8, 128), F32), ((8, 8, 128), F32), ((4, 8, 128), F32), ((4, 8, 128), F32),
        ((TOK, QRANK), BF), ((TOK, KVRANK), BF), ((TOK, 256), BF),
        ((HL, TOK, KVRANK), BF), ((HL, TOK, 256), BF), ((HL, TOK, KVRANK), BF),
        ((SLOTS, 4, CACHE, KVRANK), BF), ((SLOTS, 4, ROPE, CACHE), BF),
        ((128, CACHE), F32), ((128, 16), F32), ((128, CACHE), F32), ((128, 16), F32),
        ((4, 2, HALF, 1024), BF), ((4, 4, 2, HALF, 1024), BF),
        ((4, 4, 448, 256), BF), ((4, 2, 224, 256), BF), ((4, 2, 448, 256), BF),
        ((2, 448, 256), F32), ((8, 448, 128), BF), ((896, TOK), BF),
    ]
    counts = [
        (8,), (SLOTS,), (SLOTS,), (2,), (2,), (2,), (3,), (1,), (25,), (1,), (13,),
        (4,), (2,), (1,), (4,), (1,), (4, 2), (1,), (4,), (1,), (4,), (3,),
    ]
    return pl.pallas_call(
        layer_kernel,
        out_shape=(
            jax.ShapeDtypeStruct((896, TOK), BF), jax.ShapeDtypeStruct((TOK, TOK), BF),
            jax.ShapeDtypeStruct((1,), F32),
        ),
        in_specs=[vmem] * 4 + [smem] + [hbm] * 8,
        out_specs=(hbm, hbm, smem),
        scratch_shapes=[pltpu.VMEM(s, d) for s, d in scratch] + [dma(n) for n in counts],
        compiler_params=pltpu.CompilerParams(
            vmem_limit_bytes=67043328, collective_id=0, has_side_effects=True
        ),
        name="layer",
    )(
        ropk, slot_of, lengths.reshape(1, SEQS), frequency, lengths,
        uq, wk, wv, wo, q, latk, cache_latent, cache_rope,
    )


def shards(q_latent, new_latent, new_rope, cache_latent, cache_rope, lengths, assignment, w_uq, w_uk, w_uv, w_o):
    half = ROPE // 2
    frequency = 10000.0 ** (-np.arange(half, dtype=np.float32) / half)
    frequency = np.broadcast_to(np.tile(frequency, 4)[None, :], (8, 128)).astype(np.float32)
    held, sel, norm = layer(
        w_uq, w_uk, w_uv, w_o.T, q_latent, new_latent, new_rope.transpose(1, 2, 0), assignment,
        lengths, jnp.asarray(frequency), cache_latent, cache_rope,
    )
    out = pl.pallas_call(
        place_kernel,
        out_shape=jax.ShapeDtypeStruct((SEQS, NEWTOK, 896), BF),
        grid=(4,),
        in_specs=[
            pl.BlockSpec((128, TOK), lambda i: (i, 0)), pl.BlockSpec((896, TOK), lambda i: (0, 0))
        ],
        out_specs=pl.BlockSpec((32, NEWTOK, 896), lambda i: (i, 0, 0)),
        name="place",
    )(sel, held)
    return out, norm


def solution(mesh):
    split = Mesh(mesh.devices.reshape(4, 4, 4, 2), ("dp_0", "dp_1", "tp_0", "tp_1"))
    dp, tp = ("dp_0", "dp_1"), ("tp_0", "tp_1")
    placed = (
        P(dp, None, None), P(dp, None, None), P(dp, None, None), P(dp, None, None), P(dp, None, None),
        P(dp), P(dp, None), P(dp + tp, None), P(dp + tp, None), P(dp + tp, None), P(None, dp + tp),
    )
    return jax.shard_map(
        shards, mesh=split, in_specs=placed, out_specs=(P(dp, None, tp), P()), check_vma=False
    )
```

time: 160 us -> 141 us (0.88)
  local copies, waits for them, and re-layouts: 8.84 us -> 0 us
  Pallas kernels: 146 us -> 138 us
  other arithmetic: 4 us -> 0 us
  between operations: 0.68 us -> 2.41 us
    pallas_call x1 -> x2, Pallas kernels: 146 us -> 138 us  [the longest x1 133 us: layer(): pl.pallas_call(layer_kernel, out_shape=(jax.ShapeDtypeStruct((896, TOK),...]
    transpose x2 -> x0, local copies, waits for them, and re-layouts: 3.35 us -> none  [the longest x1 1.93 us: shards(): new_latent.transpose(1, 0, 2).reshape(TOK, KVRANK)]
    reshape x1 -> x0, local copies, waits for them, and re-layouts: 2.51 us -> none  [shards(): return (out.reshape(SEQS, NEWTOK, 896), norm[0, 0:1])]
    convert_element_type x2 -> x0, other arithmetic: 2.09 us -> none  [the longest x1 1.36 us: shards(): sel = ((jnp.repeat(slot_of, NEWTOK)[:, None] == held[None, :] // 4) & (at...]
    mul x1 -> x0, other arithmetic: 1.85 us -> none  [tables(): return (jnp.cos(angles), jnp.sin(angles) * sign[None, :])]
where the time goes in v2:
time: 141 us; the launch traced here: 140 us
  Pallas kernels  138 us (98%)
  between operations  2.41 us (2%)
    pallas_call x1, Pallas kernels, layer(): pl.pallas_call(layer_kernel, out_shape=(jax.ShapeDtypeStruct((896, TOK),...  133 us
    pallas_call x1, Pallas kernels, shards(): pl.pallas_call(place_kernel, out_shape=jax.ShapeDtypeStruct((SEQS, NEWTOK...  4.47 us

profile of v2, /device:TPU:1, one launch (start us, length us, event | category | flops | bytes accessed | tf_op | source)
XLA Modules:
  0.0 140.3 jit_solution(2157731291243111506)
XLA Ops:
  0.6 133.4 %layer.1 = (bf16[896,512]{1,0:T(8,128)(2,1)}, bf16[512,512]{1,0:T(8,128)(2,1)}, f32[1]{0:T(128)}) custom-call(bf16[4,64,128]{2,1,0:T(8,128)(2,1)} %bitcast.4, s32[1,128]{1,0:T(1,128)} %asn_ref.1, s32[1,128]{1,0:T(1,128)} %bitcast.5, f32[8,128]{1,0:T(8,128)} %constant.2.clone.freq_ref, s32[128]{0:T(128)} %len_ref.1, f32[12,12288]{1,0:T(8,128)} %uq_hbm.1, ...), custom_call_target="tpu_custom_call" | custom-call | tf_op jit(solution)/shard_map/layer/pallas_call | solution.py:715
  134.0 4.5 %place.1 = bf16[128,4,896]{2,1,0:T(4,128)(2,1)} custom-call(bf16[512,512]{1,0:T(8,128)(2,1)} %get-tuple-element.5.sel_ref, bf16[896,512]{1,0:T(8,128)(2,1)} %get-tuple-element.6.held_ref), custom_call_target="tpu_custom_call" | custom-call | tf_op jit(solution)/shard_map/place/pallas_call | solution.py:742

commit v3 on v2

--- a/solution.py
+++ b/solution.py
@@ -37,18 +37,18 @@
     return lax.dot_general(a, b, (((1,), (0,)), ((), ())), preferred_element_type=F32)
 
 
-def project(q_ref, u_ref, cos_ref, sin_ref, abs_ref, qr_ref, part):
+def project(q_ref, u_ref, cos_ref, sin_ref, abs_ref, qr_ref, part, start, count):
+    rows = pl.ds(start, count)
+
     def nope_pair(i):
         cols = pl.ds(i * 256, 256)
-        both = nn(q_ref[...], u_ref[:, 0:96, cols].reshape(QRANK, 256)).astype(BF)
+        both = nn(q_ref[rows, :], u_ref[:, 0:96, cols].reshape(QRANK, 256)).astype(BF)
         for j in range(2):
             own_cols = pl.ds(i * 256 + j * 128, 128)
             keys = u_ref[:, 96:128, own_cols].reshape(KVRANK, 128)
-            abs_ref[i * 2 + j] = nt(both[:, j * 128 : (j + 1) * 128], keys).astype(BF)
-
-    lane = lax.broadcasted_iota(jnp.int32, (TOK, 128), 1)
-    row = lax.broadcasted_iota(jnp.int32, (TOK, 128), 0)
-    own = lax.rem(row // 4, 4)
+            abs_ref[i * 2 + j, rows, :] = nt(both[:, j * 128 : (j + 1) * 128], keys).astype(BF)
+
+    lane = lax.broadcasted_iota(jnp.int32, (count, 128), 1)
     low = lax.rem(lane, 64) < 32
 
     def quad(i):
@@ -65,18 +65,13 @@
                 ],
                 axis=1,
             )
-        four = nn(q_ref[...], pe_cols).astype(BF).astype(F32)
+        four = nn(q_ref[rows, :], pe_cols).astype(BF).astype(F32)
         for j in range(2):
             pe = four[:, j * 128 : (j + 1) * 128]
             other = jnp.where(low, pltpu.roll(pe, 96, 1), pltpu.roll(pe, 32, 1))
-            rot = pe * cos_ref[...] + other * sin_ref[...]
-            flip = pltpu.roll(rot, 64, 1)
-            for odd in range(2):
-                twice = jnp.where((lane < 64) == (odd == 0), rot, flip)
-                head = i * 4 + j * 2 + odd
-                for half in range(2):
-                    kept = jnp.where(own == 2 * half + lane // 64, twice, 0.0)
-                    qr_ref[head, :, half * 128 : (half + 1) * 128] = kept.astype(BF)
+            rot = pe * cos_ref[rows, :] + other * sin_ref[rows, :]
+            qr_ref[i * 4 + j * 2, rows, :] = rot.astype(BF)
+            qr_ref[i * 4 + j * 2 + 1, rows, :] = pltpu.roll(rot, 64, 1).astype(BF)
 
     quad(part)
 
@@ -84,12 +79,14 @@
 def scores_of(g, abs_ref, qr_ref, latn_ref, ropn_ref, lat, rop, sc_ref, scn_ref):
     rows = pl.ds(pl.multiple_of(g * 16, 16), 16)
     q = abs_ref[:, rows, :].reshape(128, KVRANK)
-    qr = qr_ref[:, rows, :].reshape(128, 256)
-    seq = lax.rem(lax.broadcasted_iota(jnp.int32, (128, KVRANK), 0) // 4, 4)
-    zero = jnp.zeros_like(q)
-    parts = jnp.concatenate([jnp.where(seq == s, q, zero) for s in range(4)], axis=1)
-    keys = jnp.concatenate([lat[s] for s in range(4)], axis=1)
-    sc_ref[...] = nt(parts, keys) + nn(qr, rop[...].reshape(256, CACHE))
+    qr = qr_ref[:, rows, 0:ROPE].reshape(128, ROPE)
+    ropes = jnp.concatenate([rop[s] for s in range(4)], axis=1)
+    wide = nt(q, lat[...].reshape(4 * CACHE, KVRANK)) + nn(qr, ropes)
+    seq = lax.rem(lax.broadcasted_iota(jnp.int32, (128, CACHE), 0) // 4, 4)
+    own = wide[:, 0:CACHE]
+    for s in range(1, 4):
+        own = jnp.where(seq == s, wide[:, s * CACHE : s * CACHE + CACHE], own)
+    sc_ref[...] = own
     scn_ref[...] = nt(q, latn_ref[rows, :]) + nt(qr, ropn_ref[rows, :])
 
 
@@ -126,8 +123,8 @@
 
 
 MESH = pl.DeviceIdType.MESH
-CHUNKS = 4
-HALF = 64
+CHUNK = (64, 64, 64, 64)
+FIRST = (0, 128, 256, 384)
 
 
 def around(i, d):
@@ -241,7 +238,7 @@
         loads[n].wait()
     squares = lax.fori_loop(0, 8, pack_one, jnp.zeros((8, 128), F32))
     pl.semaphore_wait(barrier, 16)
-    for dt in range(1, 8):
+    for dt in (4, 5, 2, 3, 6, 7, 1):
         peer = lax.rem(t + dt, 8)
         send(
             packs.at[peer], rp.at[t], a2a_sem.at[0], a2a_sem.at[1], x=peer // 2, c=lax.rem(peer, 2)
@@ -257,11 +254,6 @@
     squares = lax.fori_loop(0, 8, pack_out, squares)
     nsend[0] = squares
     ntp[t] = squares
-    for dt in range(1, 8):
-        peer = lax.rem(t + dt, 8)
-        where = dict(x=peer // 2, c=lax.rem(peer, 2))
-        send(nsend.at[0], ntp.at[t], nt_sem.at[0], nt_sem.at[1], **where)
-        send(opack.at[peer], orp.at[t], o2a_sem.at[0], o2a_sem.at[1], **where)
     orp[t] = opack[t]
 
     row = lax.broadcasted_iota(jnp.int32, (TOK, TOK), 0)
@@ -386,7 +378,11 @@
         first_send(ring)
     for ring in range(2):
         second_send(ring, 0)
-
+    for dt in (4, 5, 2, 3, 6, 7, 1):
+        peer = lax.rem(t + dt, 8)
+        where = dict(x=peer // 2, c=lax.rem(peer, 2))
+        send(nsend.at[0], ntp.at[t], nt_sem.at[0], nt_sem.at[1], **where)
+        send(opack.at[peer], orp.at[t], o2a_sem.at[0], o2a_sem.at[1], **where)
     loads[4].wait()
     loads[5].wait()
     keep_sel.start()
@@ -397,54 +393,53 @@
         return carry
 
     lax.fori_loop(0, QRANK // 256, move_q, 0)
-    lax.fori_loop(0, 4, rotation, 0)
-
+    for ring in range(2):
+        first_forward(ring)
+    for ring in range(2):
+        second_send(ring, 1)
+        second_send(ring, 2)
     arrived(ntp.at[0:7], nt_sem.at[1])
     line = ntp[0]
     for i in range(1, 8):
         line = line + ntp[i]
     latn_ref[...] = nn(selk_ref[1], latk_ref[...].reshape(TOK, KVRANK)).astype(BF)
     rope_rows = jnp.concatenate([ropk_ref[k] for k in range(4)], axis=1)
-    ropn_ref[...] = nt(selk_ref[0], jnp.concatenate([rope_rows] * 4, axis=0)).astype(BF)
+    ropn_ref[...] = nt(selk_ref[0], rope_rows).astype(BF)
     nsend[1] = line
     ny[y] = line
     for d in range(1, 4):
         send(nsend.at[1], ny.at[y], nyz_sem.at[0], nyz_sem.at[1], y=around(y, d))
 
     for ring in range(2):
-        first_forward(ring)
+        second_forward(ring, 0)
     for ring in range(2):
-        second_send(ring, 1)
-        second_send(ring, 2)
+        first_last(ring)
+        second_send(ring, 3)
     first_send(2)
-    for ring in range(2):
-        second_forward(ring, 0)
+    lax.fori_loop(0, 4, rotation, 0)
     arrived(ny.at[0:3], nyz_sem.at[1])
     plane = ((ny[0] + ny[1]) + ny[2]) + ny[3]
     nsend[2] = plane
     nz[z] = plane
     for d in range(1, 4):
         send(nsend.at[2], nz.at[z], nyz_sem.at[0], nyz_sem.at[2], z=around(z, d))
-    for ring in range(2):
-        first_last(ring)
-        second_send(ring, 3)
-    first_forward(2)
     for p in range(1, 3):
         for ring in range(2):
             second_forward(ring, p)
-
     arrived(orp.at[0:7], o2a_sem.at[1])
     wo_all[c, z] = jnp.concatenate([orp[i].astype(F32) for i in range(8)], axis=0).astype(BF)
-    first_last(2)
     for ring in range(2):
         second_forward(ring, 3)
-    for p in range(4):
+    first_forward(2)
+    for p in range(3):
         second_send(2, p)
     send(wo_all.at[c, z], wo_all.at[c, z], od_sem.at[0], od_sem.at[1], c=1 - c)
     for later in range(2):
         for k, d in enumerate((1, -1)):
             part = wo_all.at[c, z, pl.ds((k ^ later) * 224, 224)]
             send(part, part, oz_sem.at[0], oz_sem.at[1 + later], z=around(z, d))
+    first_last(2)
+    second_send(2, 3)
     arrived(u_ref.at[0:4], ag_r.at[24])
     arrived(nz.at[0:3], nyz_sem.at[2])
     everything = ((nz[0] + nz[1]) + nz[2]) + nz[3]
@@ -452,11 +447,16 @@
     entries = HEADS * (NOPE + ROPE) + 2 * HEADS * NOPE + D
     norm_ref[0] = jnp.sqrt(everything / entries)[0, 0]
 
-    project(qs_ref, u_ref, cos_ref, sin_ref, abs_ref, qr_ref, 0)
+    def projected(part, start, count):
+        project(qs_ref, u_ref, cos_ref, sin_ref, abs_ref, qr_ref, part, start, count)
+
+    projected(0, 0, 144)
     second_forward(2, 0)
+    projected(1, 0, 144)
     second_forward(2, 1)
-    project(qs_ref, u_ref, cos_ref, sin_ref, abs_ref, qr_ref, 1)
-    second_forward(2, 2)
+
+    def project_rest(part):
+        projected(part, 144, TOK - 144)
 
     def score(g, sc, scn):
         slot = lax.rem(g, SLOTS)
@@ -490,8 +490,8 @@
         score(jnp.minimum(g + 2, GROUPS - 1), sc0, scn0)
         finish(g + 1, sc1, scn1)
 
-    def values_pass():
-        second_forward(2, 3)
+    def values_pass(p):
+        second_forward(2, p)
 
     def values_ready():
         arrived(v_ref.at[0:4], uv_r.at[12])
@@ -517,82 +517,105 @@
         arrived(wo_all.at[1 - c], od_sem.at[1])
 
     def head_values(j):
-        rows = slice(j * 128, j * 128 + 128)
+        n = CHUNK[j]
+        rows = slice(FIRST[j], FIRST[j] + 2 * n)
         for h in range(HL):
             up = v_ref[:, :, h * 128 : h * 128 + 128].reshape(KVRANK, 128)
             both = nn(lo_ref[h, rows, :], up).astype(BF)
             for half in range(2):
-                ho_ref[j, half, :, h * 128 : h * 128 + 128] = both[half * 64 : half * 64 + 64]
-        hb_ref[j, y, c] = ho_ref[j, c]
+                ho_ref[j, half, 0:n, h * 128 : h * 128 + 128] = both[half * n : half * n + n]
+        hb_ref[j, y, c, 0:n] = ho_ref[j, c, 0:n]
 
     def heads_done(j):
         head_values(j)
-        send(ho_ref.at[j, 1 - c], hb_ref.at[j, y, c], d2_s.at[0], d2_r.at[j], c=1 - c)
+        some = pl.ds(0, CHUNK[j])
+        target = hb_ref.at[j, y, c, some]
+        send(ho_ref.at[j, 1 - c, some], target, d2_s.at[0], d2_r.at[j], c=1 - c)
         for d in (1, -1):
-            send(ho_ref.at[j, c], hb_ref.at[j, y, c], hy_s.at[0], hy_r.at[j, 0], y=around(y, d))
+            send(ho_ref.at[j, c, some], target, hy_s.at[0], hy_r.at[j, 0], y=around(y, d))
 
     def partner_half(j):
-        ref = hb_ref.at[j, y, 1 - c]
+        ref = hb_ref.at[j, y, 1 - c, pl.ds(0, CHUNK[j])]
         arrived(ref, d2_r.at[j])
         for d in (1, -1):
             send(ref, ref, hy_s.at[0], hy_r.at[j, 0], y=around(y, d))
 
     def pass_on(j):
-        arrived(hb_ref.at[j, 0:2], hy_r.at[j, 0])
-        for k, d in enumerate((1, -1)):
-            ref = hb_ref.at[j, around(y, -d), k]
+        some = pl.ds(0, CHUNK[j])
+        arrived(hb_ref.at[j, pl.ds(0, 2), pl.ds(0, 2), some], hy_r.at[j, 0])
+        for k, d in enumerate((1, -1)):
+            ref = hb_ref.at[j, around(y, -d), k, some]
             send(ref, ref, hy_s.at[0], hy_r.at[j, 1], y=around(y, d))
 
     def multiply(j):
-        arrived(hb_ref.at[j, around(y, 2)], hy_r.at[j, 1])
-
-        def block(n):
-            zs = lax.rem(x + n, 4)
+        n = CHUNK[j]
+        lanes = pl.ds(0, 4 * n)
+        arrived(hb_ref.at[j, around(y, 2), pl.ds(0, 2), pl.ds(0, n)], hy_r.at[j, 1])
+
+        def block(m):
+            zs = lax.rem(x + m, 4)
             tokens = jnp.concatenate(
-                [hb_ref[j, :, k].reshape(4 * HALF, 1024) for k in range(2)], axis=1
+                [hb_ref[j, :, k, 0:n].reshape(4 * n, 1024) for k in range(2)], axis=1
             )
             columns = jnp.concatenate([wo_all[k, zs] for k in range(2)], axis=1)
-            ct_ref[j, zs] = nt(columns, tokens).astype(BF)
+            ct_ref[j, zs, :, 0 : 4 * n] = nt(columns, tokens).astype(BF)
 
         block(2)
         for k, d in enumerate((1, -1)):
             send(
-                ct_ref.at[j, around(x, 2), pl.ds(k * 224, 224)], r1_ref.at[j, k],
+                ct_ref.at[j, around(x, 2), pl.ds(k * 224, 224), lanes], r1_ref.at[j, k, :, lanes],
                 r1_s.at[0], r1_r.at[j], x=around(x, d),
             )
 
-        def rest(n, carry):
-            block(jnp.where(n == 0, 1, jnp.where(n == 1, 3, 0)))
+        def rest(m, carry):
+            block(jnp.where(m == 0, 1, jnp.where(m == 1, 3, 0)))
             return carry
 
         lax.fori_loop(0, 3, rest, 0)
+        for k, d in enumerate((1, -1)):
+            part = pl.ds((1 - k) * 224, 224)
+            send(
+                ct_ref.at[j, around(x, d), part, lanes], rx_ref.at[j, k, part, lanes], r2_s.at[0],
+                r2_r.at[j], x=around(x, d),
+            )
 
     def add_far(j):
-        arrived(r1_ref.at[j], r1_r.at[j])
+        n = 4 * CHUNK[j]
+        lanes = pl.ds(0, n)
+        arrived(r1_ref.at[j, :, :, lanes], r1_r.at[j])
         for k, d in enumerate((1, -1)):
             rows = slice(k * 224, k * 224 + 224)
             near = around(x, d)
-            both = ct_ref[j, near, rows].astype(F32) + r1_ref[j, k].astype(F32)
-            ct_ref[j, near, rows] = both.astype(BF)
-            send(ct_ref.at[j, near], rx_ref.at[j, k], r2_s.at[0], r2_r.at[j], x=near)
+            both = ct_ref[j, near, rows, 0:n].astype(F32) + r1_ref[j, k, :, 0:n].astype(F32)
+            ct_ref[j, near, rows, 0:n] = both.astype(BF)
+            part = pl.ds(k * 224, 224)
+            send(
+                ct_ref.at[j, near, part, lanes], rx_ref.at[j, k, part, lanes], r2_s.at[0],
+                r2_r.at[j], x=near,
+            )
 
     def collect(j):
-        fs_ref[j % 2] = (
-            ct_ref[j, x].astype(F32) + rx_ref[j, 0].astype(F32) + rx_ref[j, 1].astype(F32)
+        n = 4 * CHUNK[j]
+        total = (
+            ct_ref[j, x, :, 0:n].astype(F32)
+            + rx_ref[j, 0, :, 0:n].astype(F32)
+            + rx_ref[j, 1, :, 0:n].astype(F32)
         )
         if j % 2 == 0:
+            fs_ref[...] = total
             return
         lane = lax.broadcasted_iota(jnp.int32, (448, 128), 1)
         for v in range(2):
-            early = fs_ref[0, :, v * 128 : v * 128 + 128]
-            late = fs_ref[1, :, v * 128 : v * 128 + 128]
-            ft_ref[j // 2 * 4 + 2 * v] = jnp.where(lane < 64, early, pltpu.roll(late, 64, 1)).astype(BF)
-            ft_ref[j // 2 * 4 + 2 * v + 1] = jnp.where(lane < 64, pltpu.roll(early, 64, 1), late).astype(BF)
+            early = fs_ref[:, v * 128 : v * 128 + 128]
+            late = total[:, v * 128 : v * 128 + 128]
+            at = j // 2 * 4 + 2 * v
+            ft_ref[at] = jnp.where(lane < 64, early, pltpu.roll(late, 64, 1)).astype(BF)
+            ft_ref[at + 1] = jnp.where(lane < 64, pltpu.roll(early, 64, 1), late).astype(BF)
 
     here = y // 2 == c
 
     def add_near(j):
-        arrived(rx_ref.at[j], r2_r.at[j])
+        arrived(rx_ref.at[j, :, :, pl.ds(0, 4 * CHUNK[j])], r2_r.at[j])
         collect(j)
         if j % 2 == 0:
             return
@@ -614,22 +637,25 @@
             send(ft_ref.at[pair * 4 + y], target, f_sem.at[2], f_sem.at[1], c=1 - c)
 
     plan = {
-        0: [(values_pass,), (out_pass,)],
-        3: [(values_ready,), (heads_done, 0)],
-        4: [(partner_half, 0)],
+        0: [(values_pass, 2)],
+        1: [(values_pass, 3)],
+        3: [
+            (values_ready,), (heads_done, 0), (out_pass,), (project_rest, 0), (partner_half, 0),
+            (project_rest, 1),
+        ],
+        4: [(pass_on, 0)],
         6: [(out_near,)],
-        7: [(pass_on, 0), (heads_done, 1)],
+        7: [(heads_done, 1)],
         8: [(partner_half, 1)],
-        11: [(heads_done, 2), (out_far,)],
-        12: [(pass_on, 1), (partner_half, 2), (out_ready,), (multiply, 0)],
+        10: [(out_far,)],
+        11: [(pass_on, 1), (heads_done, 2), (out_ready,), (multiply, 0)],
+        12: [(partner_half, 2)],
         13: [(add_far, 0)],
-        14: [(multiply, 1)],
         15: [(pass_on, 2), (heads_done, 3)],
-        16: [(add_near, 0), (partner_half, 3), (add_far, 1)],
-        17: [(multiply, 2)],
-        18: [(pass_on, 3), (add_near, 1), (add_far, 2)],
-        19: [(multiply, 3)],
-        20: [(add_near, 2), (add_far, 3), (add_near, 3)],
+        16: [(add_near, 0), (partner_half, 3)],
+        17: [(multiply, 1), (multiply, 2)],
+        18: [(add_far, 1), (pass_on, 3), (add_far, 2)],
+        19: [(multiply, 3), (add_near, 1), (add_near, 2), (add_far, 3), (add_near, 3)],
     }
 
     def run(events):
@@ -648,7 +674,7 @@
         return carry
 
     lax.fori_loop(0, 16, together, 0)
-    for slot in range(16, 21):
+    for slot in range(16, 20):
         run(plan[slot])
 
     @pl.when(here)
@@ -682,11 +708,6 @@
     keep_out.wait()
 
 
-def place_kernel(sel_ref, held_ref, out_ref):
-    placed = nt(sel_ref[...], held_ref[...]).astype(BF)
-    out_ref[...] = placed.reshape(32, 4, 896)
-
-
 def layer(uq, wk, wv, wo, q, latk, ropk, slot_of, lengths, frequency, cache_latent, cache_rope):
     vmem = pl.BlockSpec(memory_space=pltpu.VMEM)
     smem = pl.BlockSpec(memory_space=pltpu.SMEM)
@@ -700,13 +721,13 @@
         ((8, 56, 1024), BF), ((8, 56, 1024), BF),
         ((16, 128, 1408), BF), ((16, 32, 1024), BF), ((2, 4, 448, 1024), BF),
         ((3, 8, 128), F32), ((8, 8, 128), F32), ((4, 8, 128), F32), ((4, 8, 128), F32),
-        ((TOK, QRANK), BF), ((TOK, KVRANK), BF), ((TOK, 256), BF),
-        ((HL, TOK, KVRANK), BF), ((HL, TOK, 256), BF), ((HL, TOK, KVRANK), BF),
+        ((TOK, QRANK), BF), ((TOK, KVRANK), BF), ((TOK, ROPE), BF),
+        ((HL, TOK, KVRANK), BF), ((HL, TOK, 128), BF), ((HL, TOK, KVRANK), BF),
         ((SLOTS, 4, CACHE, KVRANK), BF), ((SLOTS, 4, ROPE, CACHE), BF),
         ((128, CACHE), F32), ((128, 16), F32), ((128, CACHE), F32), ((128, 16), F32),
-        ((4, 2, HALF, 1024), BF), ((4, 4, 2, HALF, 1024), BF),
+        ((4, 2, 64, 1024), BF), ((4, 4, 2, 64, 1024), BF),
         ((4, 4, 448, 256), BF), ((4, 2, 224, 256), BF), ((4, 2, 448, 256), BF),
-        ((2, 448, 256), F32), ((8, 448, 128), BF), ((896, TOK), BF),
+        ((448, 256), F32), ((8, 448, 128), BF), ((896, TOK), BF),
     ]
     counts = [
         (8,), (SLOTS,), (SLOTS,), (2,), (2,), (2,), (3,), (1,), (25,), (1,), (13,),
@@ -739,16 +760,7 @@
         w_uq, w_uk, w_uv, w_o.T, q_latent, new_latent, new_rope.transpose(1, 2, 0), assignment,
         lengths, jnp.asarray(frequency), cache_latent, cache_rope,
     )
-    out = pl.pallas_call(
-        place_kernel,
-        out_shape=jax.ShapeDtypeStruct((SEQS, NEWTOK, 896), BF),
-        grid=(4,),
-        in_specs=[
-            pl.BlockSpec((128, TOK), lambda i: (i, 0)), pl.BlockSpec((896, TOK), lambda i: (0, 0))
-        ],
-        out_specs=pl.BlockSpec((32, NEWTOK, 896), lambda i: (i, 0, 0)),
-        name="place",
-    )(sel, held)
+    out = nt(sel, held).astype(BF).reshape(SEQS, NEWTOK, 896)
     return out, norm
 
 

time: 141 us -> 134 us (0.950)
  Pallas kernels: 138 us -> 129 us
  matrix products: 0 us -> 2.08 us
    pallas_call x1, Pallas kernels: 133 us -> 129 us  [layer(): pl.pallas_call(layer_kernel, out_shape=(jax.ShapeDtypeStruct((896, TOK),...]
    pallas_call x1 -> x0, Pallas kernels: 4.47 us -> none  [shards(): pl.pallas_call(place_kernel, out_shape=jax.ShapeDtypeStruct((SEQS, NEWTOK...]
    dot_general x0 -> x1, matrix products: none -> 2.08 us  [nt(): lax.dot_general(a, b, (((1,), (1,)), ((), ())), preferred_element_type=F32)]
where the time goes in v3:
time: 134 us
  Pallas kernels  129 us (96%)
  between operations  2.41 us (2%)
  matrix products  2.08 us (2%)
    pallas_call x1, Pallas kernels, layer(): pl.pallas_call(layer_kernel, out_shape=(jax.ShapeDtypeStruct((896, TOK),...  129 us

profile of v3, /device:TPU:1, one launch (start us, length us, event | category | flops | bytes accessed | tf_op | source)
XLA Modules:
  0.0 134.2 jit_solution(15366572007727377516)
XLA Ops:
  0.6 128.6 %layer.1 = (bf16[896,512]{1,0:T(8,128)(2,1)}, bf16[512,512]{1,0:T(8,128)(2,1)}, f32[1]{0:T(128)}) custom-call(bf16[4,64,128]{2,1,0:T(8,128)(2,1)} %bitcast.6, s32[1,128]{1,0:T(1,128)} %asn_ref.1, s32[1,128]{1,0:T(1,128)} %bitcast.7, f32[8,128]{1,0:T(8,128)} %constant.2.clone.freq_ref, s32[128]{0:T(128)} %len_ref.1, f32[12,12288]{1,0:T(8,128)} %uq_hbm.1, ...), custom_call_target="tpu_custom_call" | custom-call | tf_op jit(solution)/shard_map/layer/pallas_call | solution.py:736
  129.2 2.1 %convolution_convert_fusion = bf16[512,896]{1,0:T(8,128)(2,1)S(1)} fusion(bf16[512,512]{1,0:T(8,128)(2,1)} %get-tuple-element.5, bf16[896,512]{1,0:T(8,128)(2,1)} %get-tuple-element.6), kind=kOutput, calls=%fused_computation | convolution fusion | flops 470220800 | bytes 2359296 | tf_op jit(solution)/shard_map/dot_general | solution.py:33
  131.3 1.1 reshape.11

commit v4 on v3

--- a/solution.py
+++ b/solution.py
@@ -547,28 +547,31 @@
             ref = hb_ref.at[j, around(y, -d), k, some]
             send(ref, ref, hy_s.at[0], hy_r.at[j, 1], y=around(y, d))
 
-    def multiply(j):
+    def product(j, zs):
+        n = CHUNK[j]
+        tokens = jnp.concatenate(
+            [hb_ref[j, :, k, 0:n].reshape(4 * n, 1024) for k in range(2)], axis=1
+        )
+        columns = jnp.concatenate([wo_all[k, zs] for k in range(2)], axis=1)
+        ct_ref[j, zs, :, 0 : 4 * n] = nt(columns, tokens).astype(BF)
+
+    def multiply_far(j):
         n = CHUNK[j]
         lanes = pl.ds(0, 4 * n)
         arrived(hb_ref.at[j, around(y, 2), pl.ds(0, 2), pl.ds(0, n)], hy_r.at[j, 1])
 
-        def block(m):
-            zs = lax.rem(x + m, 4)
-            tokens = jnp.concatenate(
-                [hb_ref[j, :, k, 0:n].reshape(4 * n, 1024) for k in range(2)], axis=1
-            )
-            columns = jnp.concatenate([wo_all[k, zs] for k in range(2)], axis=1)
-            ct_ref[j, zs, :, 0 : 4 * n] = nt(columns, tokens).astype(BF)
-
-        block(2)
+        product(j, lax.rem(x + 2, 4))
         for k, d in enumerate((1, -1)):
             send(
                 ct_ref.at[j, around(x, 2), pl.ds(k * 224, 224), lanes], r1_ref.at[j, k, :, lanes],
                 r1_s.at[0], r1_r.at[j], x=around(x, d),
             )
 
+    def multiply_near(j):
+        lanes = pl.ds(0, 4 * CHUNK[j])
+
         def rest(m, carry):
-            block(jnp.where(m == 0, 1, jnp.where(m == 1, 3, 0)))
+            product(j, lax.rem(x + jnp.where(m == 0, 1, jnp.where(m == 1, 3, 0)), 4))
             return carry
 
         lax.fori_loop(0, 3, rest, 0)
@@ -578,6 +581,10 @@
                 ct_ref.at[j, around(x, d), part, lanes], rx_ref.at[j, k, part, lanes], r2_s.at[0],
                 r2_r.at[j], x=around(x, d),
             )
+
+    def multiply(j):
+        multiply_far(j)
+        multiply_near(j)
 
     def add_far(j):
         n = 4 * CHUNK[j]
@@ -650,12 +657,12 @@
         10: [(out_far,)],
         11: [(pass_on, 1), (heads_done, 2), (out_ready,), (multiply, 0)],
         12: [(partner_half, 2)],
-        13: [(add_far, 0)],
+        13: [(add_far, 0), (multiply_far, 1)],
         15: [(pass_on, 2), (heads_done, 3)],
-        16: [(add_near, 0), (partner_half, 3)],
-        17: [(multiply, 1), (multiply, 2)],
-        18: [(add_far, 1), (pass_on, 3), (add_far, 2)],
-        19: [(multiply, 3), (add_near, 1), (add_near, 2), (add_far, 3), (add_near, 3)],
+        16: [(add_near, 0), (partner_half, 3), (multiply_near, 1), (add_far, 1)],
+        17: [(multiply, 2)],
+        18: [(pass_on, 3), (add_far, 2), (add_near, 1)],
+        19: [(multiply, 3), (add_near, 2), (add_far, 3), (add_near, 3)],
     }
 
     def run(events):

time: 134 us -> 133 us (level)
  Pallas kernels: 129 us -> 127 us
    pallas_call x1, Pallas kernels: 129 us -> 127 us  [layer(): pl.pallas_call(layer_kernel, out_shape=(jax.ShapeDtypeStruct((896, TOK),...]
where the time goes in v4:
time: 133 us; the launch traced here: 132 us
  Pallas kernels  127 us (95%)
  between operations  2.41 us (2%)
  matrix products  2.08 us (2%)
    pallas_call x1, Pallas kernels, layer(): pl.pallas_call(layer_kernel, out_shape=(jax.ShapeDtypeStruct((896, TOK),...  127 us

profile of v4, /device:TPU:1, one launch (start us, length us, event | category | flops | bytes accessed | tf_op | source)
XLA Modules:
  0.0 132.4 jit_solution(2268784965985048998)
XLA Ops:
  0.6 126.8 %layer.1 = (bf16[896,512]{1,0:T(8,128)(2,1)}, bf16[512,512]{1,0:T(8,128)(2,1)}, f32[1]{0:T(128)}) custom-call(bf16[4,64,128]{2,1,0:T(8,128)(2,1)} %bitcast.6, s32[1,128]{1,0:T(1,128)} %asn_ref.1, s32[1,128]{1,0:T(1,128)} %bitcast.7, f32[8,128]{1,0:T(8,128)} %constant.2.clone.freq_ref, s32[128]{0:T(128)} %len_ref.1, f32[12,12288]{1,0:T(8,128)} %uq_hbm.1, ...), custom_call_target="tpu_custom_call" | custom-call | tf_op jit(solution)/shard_map/layer/pallas_call | solution.py:743
  127.4 2.1 %convolution_convert_fusion = bf16[512,896]{1,0:T(8,128)(2,1)S(1)} fusion(bf16[512,512]{1,0:T(8,128)(2,1)} %get-tuple-element.5, bf16[896,512]{1,0:T(8,128)(2,1)} %get-tuple-element.6), kind=kOutput, calls=%fused_computation | convolution fusion | flops 470220800 | bytes 2359296 | tf_op jit(solution)/shard_map/dot_general | solution.py:33
  129.5 1.1 reshape.11
